TPU v7x, 128 devices: a whole 4x4x4 slice. The times are simulated.
128 devices in a mesh: seq: 16 (over y, x), tensor: 8 (over z, core).
Axes of the slice: x: 4, y: 4, z: 4, core: 2. Of those that a mesh axis runs over, the one named last changes fastest.
Arguments:
- tokens: bfloat16 [8192, 2048], P('seq'), may hold values from -200 to 200
- w_latent: bfloat16 [2048, 512], P(None, 'tensor'), may hold values from -0.125 to 0.125
- w_query: bfloat16 [2048, 2048], P(None, 'tensor'), may hold values from -0.125 to 0.125
- w_key_up: bfloat16 [512, 2048], P(None, 'tensor'), may hold values from -0.25 to 0.25
- w_value_up: bfloat16 [512, 2048], P(None, 'tensor'), may hold values from -0.25 to 0.25
- w_stu_query: bfloat16 [2048, 2048], P(None, 'tensor'), may hold values from -0.125 to 0.125
- w_stu_key: bfloat16 [2048, 2048], P(None, 'tensor'), may hold values from -0.125 to 0.125
- w_stu_value: bfloat16 [2048, 2048], P(None, 'tensor'), may hold values from -0.125 to 0.125
- forget: float32 [8192, 16], P('seq', 'tensor'), may hold values from -1 to 0
Outputs:
- teacher_out: bfloat16 [8192, 2048], P('seq', 'tensor')
- loss_mean: float32 [], replicated
- weight_grad: float32 [2048, 2048], P('seq', 'tensor')
All inputs are finite; a program needn't handle non-finite values.
Results may differ from a plain program's by a relative error of at most 0.02.
The roundings to bfloat16 on the way count: a program that leaves them out, or rounds other values in their place, can miss the bound.
Values may be sent and summed in bfloat16 or wider, within the bound.
A program may use at most 64 MiB of HBM per device.

v0:
```python
import math

import jax
import jax.numpy as jnp
from jax import lax
from jax.sharding import Mesh
from jax.sharding import PartitionSpec as P

SEQ = ("seq_0", "seq_1")
TENSOR = ("tensor_0", "tensor_1")
SEQ_TENSOR = ("seq_0", "seq_1", "tensor_0", "tensor_1")


NEG_FILL = -1e30
EPSILON = 1e-06


def laid_out(tiles, dim):
    lengths = list(tiles.shape[1:])
    lengths[dim] *= tiles.shape[0]
    return jnp.moveaxis(tiles, 0, dim).reshape(lengths)


def copy_for_each(value, axis):
    devices = lax.axis_size(axis)
    return lax.all_to_all(
        jnp.broadcast_to(value[None], (devices, *value.shape)), axis, 0, 0, tiled=True
    )


def gathered_copies(value, axis, dim):
    return laid_out(copy_for_each(value, axis), dim)


def side_by_side(arrays, axis, dim, along):
    both = jnp.concatenate(arrays, axis=along)
    result, at, gathered = (lax.all_gather(both, axis, axis=dim, tiled=True), 0, [])
    for a in arrays:
        gathered.append(lax.slice_in_dim(result, at, at + a.shape[along], axis=along))
        at += a.shape[along]
    return tuple(gathered)


def filled_with(value, identity):
    return jax.tree.map(
        lambda a, e: jnp.broadcast_to(jnp.asarray(e, a.dtype), a.shape), value, identity
    )


def entering(value, axes, combine, identity):
    before = start = filled_with(value, identity)
    running = value
    for axis in reversed(axes):
        devices, position = (lax.axis_size(axis), lax.axis_index(axis))
        pieces = jax.tree.map(
            lambda part, kind: lax.all_gather(part.astype(kind), axis),
            running,
            (jnp.bfloat16, jnp.bfloat16),
        )
        inside, running = (start, start)
        for k in range(devices):
            passed = k < position
            running = combine(
                running, jax.tree.map(lambda part, own: part[k].astype(own.dtype), pieces, value)
            )
            inside = jax.tree.map(lambda new, old: jnp.where(passed, new, old), running, inside)
        before = combine(inside, before)
    return before


def by_axis(value, axes):
    for axis in axes:
        value = lax.psum(value, axis)
    return value


def carried_in(value, axes, combine, identity):
    before = start = filled_with(value, identity)
    running = value
    for axis in reversed(axes):
        devices, position = (lax.axis_size(axis), lax.axis_index(axis))
        pieces = jax.tree.map(
            lambda part, kind: lax.all_gather(part.astype(kind), axis),
            running,
            jax.tree.map(lambda a: jnp.bfloat16 if a.dtype == jnp.float32 else a.dtype, value),
        )
        inside, running = (start, start)
        for k in reversed(range(devices)):
            passed = k > position
            running = combine(
                running, jax.tree.map(lambda part, own: part[k].astype(own.dtype), pieces, value)
            )
            inside = jax.tree.map(lambda new, old: jnp.where(passed, new, old), running, inside)
        before = combine(inside, before)
    return before


def split_up(value, dim, devices):
    before, after = (value.shape[:dim], value.shape[dim + 1 :])
    return jnp.moveaxis(value.reshape(*before, devices, -1, *after), dim, 0)


def sum_at_owner(value, axis, dim):
    devices = lax.axis_size(axis)
    tiles = lax.all_to_all(split_up(value, dim, devices), axis, 0, 0, tiled=True)
    return jnp.sum(tiles.astype(jnp.float32), axis=0)


def split_heads(matrix, heads_local):
    return matrix.reshape(matrix.shape[0], heads_local, matrix.shape[1] // heads_local)


def unit_rows(matrix):
    return matrix * lax.rsqrt(jnp.sum(matrix * matrix, axis=-1, keepdims=True) + EPSILON)


def chain_states(earlier, later):
    return (earlier[0] * later[0], later[0][:, None, None] * earlier[1] + later[1])


def fold_blocks(running, arrays, step):
    all_rows = arrays[0].shape[0]
    block_size = math.gcd(all_rows, 512)
    block_count = all_rows // block_size
    stacked = tuple(
        (member.reshape((block_count, block_size) + member.shape[1:]) for member in arrays)
    )

    def one_block(carried, inputs):
        return (step(carried, inputs[1], inputs[0] * block_size), None)

    block_ids = jnp.arange(block_count, dtype=jnp.int32)
    return lax.scan(one_block, running, (block_ids, stacked))[0]


def per_device(
    tokens, w_latent, w_query, w_key_up, w_value_up, w_stu_query, w_stu_key, w_stu_value, forget
):
    highest = lax.Precision.HIGHEST
    tok_rows = tokens.shape[0]
    heads_local = forget.shape[1]
    head_size = w_query.shape[1] // heads_local
    score_scale = 1.0 / math.sqrt(head_size)
    seq_count = lax.axis_size(SEQ)
    seq_index = lax.axis_index(SEQ)
    positions = seq_index * tok_rows + jnp.arange(tok_rows, dtype=jnp.int32)
    latent_part = jnp.dot(tokens, w_latent, preferred_element_type=jnp.float32).astype(jnp.bfloat16)
    latent = gathered_copies(latent_part, TENSOR, 1)
    queries = split_heads(
        jnp.dot(tokens, w_query, preferred_element_type=jnp.float32).astype(jnp.bfloat16),
        heads_local,
    )

    def attend(running, key_rows, value_rows, first_row):
        row_best, row_total, weighted = running
        key_count = key_rows.shape[0]
        key_heads = split_heads(key_rows, heads_local)
        value_heads = split_heads(value_rows, heads_local)
        scores = (
            jnp.einsum("qhd,khd->hqk", queries, key_heads, preferred_element_type=jnp.float32)
            * score_scale
        )
        allowed = (first_row + jnp.arange(key_count, dtype=jnp.int32))[None, :] <= positions[
            :, None
        ]
        scores = jnp.where(allowed[None], scores, NEG_FILL)
        new_best = jnp.maximum(row_best, jnp.max(scores, axis=2))
        weights = jnp.where(allowed[None], jnp.exp(scores - new_best[:, :, None]), 0.0)
        factor = jnp.exp(row_best - new_best)
        row_total = row_total * factor + jnp.sum(weights, axis=2)
        weighted = weighted * factor[:, :, None] + jnp.einsum(
            "hqk,khd->hqd",
            weights.astype(jnp.bfloat16),
            value_heads,
            preferred_element_type=jnp.float32,
        )
        return (new_best, row_total, weighted)

    starting = (
        jnp.full((heads_local, tok_rows), NEG_FILL, jnp.float32),
        jnp.zeros((heads_local, tok_rows), jnp.float32),
        jnp.zeros((heads_local, tok_rows, head_size), jnp.float32),
    )
    own_keys = jnp.dot(latent, w_key_up, preferred_element_type=jnp.float32).astype(jnp.bfloat16)
    own_values = jnp.dot(latent, w_value_up, preferred_element_type=jnp.float32).astype(
        jnp.bfloat16
    )

    def pair_step(carried, blocks, first_row):
        return attend(carried, blocks[0], blocks[1], first_row)

    finished = fold_blocks(starting, side_by_side((own_keys, own_values), SEQ, 0, 1), pair_step)
    teacher_heads = finished[2] / finished[1][:, :, None]
    teacher_out = (
        jnp.transpose(teacher_heads, (1, 0, 2))
        .reshape(tok_rows, heads_local * head_size)
        .astype(jnp.bfloat16)
    )
    stu_query = unit_rows(
        split_heads(jnp.dot(tokens, w_stu_query, preferred_element_type=jnp.float32), heads_local)
    )
    stu_key = unit_rows(
        split_heads(jnp.dot(tokens, w_stu_key, preferred_element_type=jnp.float32), heads_local)
    )
    stu_value = split_heads(
        jnp.dot(tokens, w_stu_value, preferred_element_type=jnp.float32), heads_local
    )
    log_cumul = jnp.cumsum(forget, axis=0).T
    causal = positions[None, :] <= positions[:, None]
    log_gap = log_cumul[:, :, None] - log_cumul[:, None, :]
    decays = jnp.exp(jnp.where(causal[None], log_gap, NEG_FILL))
    mixing = jnp.einsum("qhd,khd->hqk", stu_query, stu_key, precision=highest) * decays
    intra_out = jnp.einsum("hqk,khd->qhd", mixing, stu_value, precision=highest)
    block_end = log_cumul[:, -1]
    end_weights = jnp.exp(block_end[:, None] - log_cumul)
    state_end = jnp.einsum(
        "khd,khe->hde", stu_key * end_weights.T[:, :, None], stu_value, precision=highest
    )
    carry_decay = jnp.exp(block_end)
    start_weights = jnp.exp(log_cumul).T
    prefix = entering(
        (carry_decay, state_end),
        SEQ,
        chain_states,
        (jnp.ones_like(carry_decay), jnp.zeros_like(state_end)),
    )[1]
    cross_out = start_weights[:, :, None] * jnp.einsum(
        "qhd,hde->qhe", stu_query, prefix, precision=highest
    )
    student_out = intra_out + cross_out
    mismatch = student_out - split_heads(teacher_out.astype(jnp.float32), heads_local)
    total_rows = seq_count * tok_rows
    loss_sum = by_axis(jnp.sum(mismatch * mismatch), SEQ_TENSOR)
    loss_mean = loss_sum / (2.0 * total_rows * heads_local * lax.axis_size(TENSOR) * head_size)
    grad_out = mismatch / math.sqrt(total_rows)
    back_intra = jnp.einsum("hqk,qhd->khd", mixing, grad_out, precision=highest)
    back_state = jnp.einsum(
        "qhd,qhe->hde", stu_query * start_weights[:, :, None], grad_out, precision=highest
    )
    suffix = carried_in(
        (carry_decay, back_state),
        SEQ,
        chain_states,
        (jnp.ones_like(carry_decay), jnp.zeros_like(back_state)),
    )[1]
    back_cross = end_weights.T[:, :, None] * jnp.einsum(
        "khd,hde->khe", stu_key, suffix, precision=highest
    )
    value_grad = (
        (back_intra + back_cross).reshape(tok_rows, heads_local * head_size).astype(jnp.bfloat16)
    )
    weight_grad = sum_at_owner(
        lax.dot_general(
            tokens, value_grad, (((0,), (0,)), ((), ())), preferred_element_type=jnp.float32
        ).astype(jnp.bfloat16),
        SEQ,
        0,
    )
    return (teacher_out, loss_mean, weight_grad)


def solution(mesh):
    finer = Mesh(mesh.devices.reshape(4, 4, 4, 2), ("seq_0", "seq_1", "tensor_0", "tensor_1"))
    placed = (
        P(SEQ, None),
        P(None, TENSOR),
        P(None, TENSOR),
        P(None, TENSOR),
        P(None, TENSOR),
        P(None, TENSOR),
        P(None, TENSOR),
        P(None, TENSOR),
        P(SEQ, TENSOR),
    )
    return jax.shard_map(
        per_device,
        mesh=finer,
        in_specs=placed,
        out_specs=(P(SEQ, TENSOR), P(), P(SEQ, TENSOR)),
        check_vma=False,
    )
```

profile of v0, /device:TPU:0, one launch (start us, length us, event | category | flops | bytes accessed | tf_op | source)
XLA Modules:
  0.0 330.7 jit_solution(11338741456241015788)
XLA Ops:
  10.5 15.6 %all_to_all.10 = bf16[8,512,64]{1,2,0:T(8,128)(2,1)S(1)} all-to-all(bf16[8,512,64]{1,2,0:T(8,128)(2,1)S(1)} %broadcast_in_dim.43), channel_id=1, replica_groups=mesh['seq_0'=4,'seq_1'=4,'tensor_0'=4,'tensor_1'=2] {'tensor_0','tensor_1'}, dimensions={0} | all-to-all | bytes 1048576 | tf_op jit(solution)/shard_map/all_to_all | solution.py:26
  30.5 10.5 %all-reduce = bf16[8]{0:T(256)(128)(2,1)S(1)} all-reduce(bf16[8]{0:T(256)(128)(2,1)S(1)} %dynamic-update-slice), channel_id=2, replica_groups=mesh['seq_0'=4,'seq_1'=4,'tensor_0'=4,'tensor_1'=2] {'seq_1'}, use_global_device_ids=true, to_apply=%add | all-reduce | flops 8 | bytes 32
  41.0 10.0 %all-gather.3 = bf16[4,1,2]{2,1,0:T(2,128)(2,1)S(1)} all-gather(bf16[1,1,2]{2,1,0:T(2,128)(2,1)S(1)} %get-tuple-element.163), channel_id=1, replica_groups=mesh['seq_0'=4,'seq_1'=4,'tensor_0'=4,'tensor_1'=2] {'seq_0'}, dimensions={0}, use_global_device_ids=true | all-gather | bytes 20 | tf_op jit(solution)/shard_map/all_gather | solution.py:56
  51.0 7.0 %all-gather.4 = bf16[4,1,2]{2,1,0:T(2,128)(2,1)S(1)} all-gather(bf16[1,1,2]{2,1,0:T(2,128)(2,1)S(1)} %get-tuple-element.162), channel_id=1, replica_groups=mesh['seq_0'=4,'seq_1'=4,'tensor_0'=4,'tensor_1'=2] {'seq_0'}, dimensions={0}, use_global_device_ids=true | all-gather | bytes 20 | tf_op jit(solution)/shard_map/all_gather | solution.py:83
  63.8 13.6 %all-gather.1 = bf16[8,128,128]{2,1,0:T(8,128)(2,1)S(1)} all-gather(bf16[2,128,128]{2,1,0:T(8,128)(2,1)S(1)} %convolution_convert_fusion.5), channel_id=3, replica_groups=mesh['seq_0'=4,'seq_1'=4,'tensor_0'=4,'tensor_1'=2] {'seq_1'}, dimensions={0}, use_global_device_ids=true | all-gather | bytes 327680 | tf_op jit(solution)/shard_map/all_gather | solution.py:56
  77.7 13.7 %all_gather.42 = bf16[4,2,128,128]{3,2,1,0:T(8,128)(2,1)S(1)} all-gather(bf16[1,2,128,128]{3,2,1,0:T(8,128)(2,1)S(1)} %fusion.63), channel_id=1, replica_groups=mesh['seq_0'=4,'seq_1'=4,'tensor_0'=4,'tensor_1'=2] {'seq_0'}, dimensions={0}, use_global_device_ids=true | all-gather | bytes 327680 | tf_op jit(solution)/shard_map/all_gather | solution.py:56
  94.1 3.6 %exponential_multiply_fusion = f32[2,512,512]{2,1,0:T(8,128)} fusion(f32[2,512]{1,0:T(2,128)S(1)} %bitcast.317, pred[512,512]{1,0:T(8,128)(4,1)S(1)} %broadcast_compare_fusion.1, f32[512,2,128]{0,2,1:T(8,128)S(1)} %bitcast.309, f32[512,2,128]{0,2,1:T(8,128)S(1)} %bitcast.312, f32[512,2]{0,1:T(2,128)S(1)} %add_rsqrt_fusion, f32[512,2]{0,1:T(2,128)S(1)} %add_rsqrt_fusion.1), kind=kOutput, calls=%fused_computation.29 | convolution fusion | flops 807141376 | bytes 3420160 | tf_op jit(solution)/shard_map/qhd,khd->hqk/dot_general | solution.py:212
  97.7 8.5 %all-gather.7.cloned.1.call-done = bf16[8192,512]{0,1:T(8,128)(2,1)} async-done(((bf16[512,512]{0,1:T(8,128)(2,1)}), bf16[8192,512]{0,1:T(8,128)(2,1)}) %all-gather.7.cloned.1.call-update) | async-done | bytes 8388624 | tf_op jit(solution)/shard_map/all_gather | solution.py:37
  106.2 3.9 %fusion.158 = (bf16[8192,256]{0,1:T(8,128)(2,1)S(1)}, bf16[8192,256]{0,1:T(8,128)(2,1)S(1)}) fusion(bf16[8192,512]{0,1:T(8,128)(2,1)} %all-gather.7.cloned.1.call-done), kind=kLoop, calls=%fused_computation.252 | loop fusion | bytes 16777216 | tf_op jit(solution)/shard_map/slice | solution.py:39
  110.1 4.2 %copy_bitcast_fusion = (bf16[16,512,256]{1,2,0:T(8,128)(2,1)}, bf16[16,512,256]{1,2,0:T(8,128)(2,1)}) fusion(bf16[32,16,8,512]{3,2,1,0:T(8,128)(2,1)S(1)} %bitcast.299, bf16[32,16,8,512]{3,2,1,0:T(8,128)(2,1)S(1)} %bitcast.300), kind=kLoop, calls=%fused_computation.25 | loop fusion | bytes 16777216
  114.3 127.0 %while.15 = (s32[]{:T(128)}, f32[2,512]{1,0:T(2,128)S(1)}, f32[2,512]{1,0:T(2,128)S(1)}, f32[2,512,128]{2,1,0:T(8,128)S(1)}, s32[16]{0:T(128)S(1)}, /*index=5*/b...) while((s32[]{:T(128)}, f32[2,512]{1,0:T(2,128)S(1)}, ...), condition=%wide.region_3.4_spmd.clone, body=%wide.region_0.3_spmd.clone.sunk | while | flops 275912704 | bytes 18686152 | solution.py:133
  118.8 2.3 fusion.197
  142.6 2.3 fusion.197
  166.4 2.3 fusion.197
  174.3 2.3 fusion.197
  229.9 2.3 fusion.197
  243.5 4.7 %multiply_reduce_fusion = (f32[]{:T(128)}, f32[512,2,128]{0,2,1:T(8,128)S(1)}) fusion(bf16[2,512,128]{1,2,0:T(8,128)(2,1)S(1)} %divide_convert_fusion, f32[512,2,128]{0,2,1:T(8,128)} %fusion.19, f32[512,2,128]{0,2,1:T(8,128)S(1)} %bitcast.307, f32[2,512,512]{2,1,0:T(8,128)} %exponential_multiply_fusion), kind=kOutput, calls=%fused_computation.50 | convolution fusion | flops 805961728 | bytes 3932164 | tf_op jit(solution)/shard_map/hqk,khd->qhd/dot_general | solution.py:213
  248.9 12.3 %all-gather.2 = bf16[8,128,128]{2,1,0:T(8,128)(2,1)S(1)} all-gather(bf16[2,128,128]{2,1,0:T(8,128)(2,1)S(1)} %convolution_convert_fusion.4), channel_id=4, replica_groups=mesh['seq_0'=4,'seq_1'=4,'tensor_0'=4,'tensor_1'=2] {'seq_1'}, dimensions={0}, use_global_device_ids=true | all-gather | bytes 327680 | tf_op jit(solution)/shard_map/all_gather | solution.py:83
  261.2 12.6 %all_gather.46 = bf16[4,2,128,128]{3,2,1,0:T(8,128)(2,1)S(1)} all-gather(bf16[1,2,128,128]{3,2,1,0:T(8,128)(2,1)S(1)} %fusion.71), channel_id=1, replica_groups=mesh['seq_0'=4,'seq_1'=4,'tensor_0'=4,'tensor_1'=2] {'seq_0'}, dimensions={0}, use_global_device_ids=true | all-gather | bytes 327680 | tf_op jit(solution)/shard_map/all_gather | solution.py:83
  278.0 4.7 %all-to-all-start.1 = ((bf16[16,128,256]{1,2,0:T(8,128)(2,1)}), bf16[16,128,256]{1,2,0:T(8,128)(2,1)S(1)}, u32[]{:S(2)}, u32[]{:S(2)}) async-start(bf16[16,128,256]{1,2,0:T(8,128)(2,1)} %bitcast.304), calls=%async_computation.1 | async-start | bytes 2097152 | tf_op jit(solution)/shard_map/all_to_all | solution.py:105
  282.8 11.9 %psum.28 = f32[]{:T(128)} all-reduce(f32[]{:T(128)} %get-tuple-element.172), channel_id=1, replica_groups=mesh['seq_0'=4,'seq_1'=4,'tensor_0'=4,'tensor_1'=2] {'seq_0'}, use_global_device_ids=true, to_apply=%region_9.10 | all-reduce | flops 1 | bytes 8 | tf_op jit(solution)/shard_map/psum | solution.py:73
  294.7 11.0 %psum.29 = f32[]{:T(128)} all-reduce(f32[]{:T(128)} %psum.28), channel_id=1, replica_groups=mesh['seq_0'=4,'seq_1'=4,'tensor_0'=4,'tensor_1'=2] {'seq_1'}, use_global_device_ids=true, to_apply=%region_10.11 | all-reduce | flops 1 | bytes 8 | tf_op jit(solution)/shard_map/psum | solution.py:73
  305.7 11.5 %psum.30 = f32[]{:T(128)} all-reduce(f32[]{:T(128)} %psum.29), channel_id=1, replica_groups=mesh['seq_0'=4,'seq_1'=4,'tensor_0'=4,'tensor_1'=2] {'tensor_0'}, use_global_device_ids=true, to_apply=%region_11.12 | all-reduce | flops 1 | bytes 8 | tf_op jit(solution)/shard_map/psum | solution.py:73
  317.2 3.1 psum.31
  (272 shorter events, 128.7 us)
Async XLA Ops:
  7.2 18.9 %copy-start.10 = (bf16[512,256]{1,0:T(8,128)(2,1)S(1)}, bf16[512,256]{1,0:T(8,128)(2,1)}, u32[]{:S(2)}) copy-start(bf16[512,256]{1,0:T(8,128)(2,1)} %param.15) | copy-start | bytes 786436
  7.2 19.3 %copy-start.11 = (bf16[512,256]{1,0:T(8,128)(2,1)S(1)}, bf16[512,256]{1,0:T(8,128)(2,1)}, u32[]{:S(2)}) copy-start(bf16[512,256]{1,0:T(8,128)(2,1)} %param.14) | copy-start | bytes 786436
  7.2 99.0 %all-gather.7.cloned.1.call-start = ((), (), s32[]{:S(2)}) async-start(), calls=%async_computation.2 | async-start | bytes 8912896 | tf_op jit(solution)/shard_map/all_gather | solution.py:37
  26.1 2.9 copy-start.15
  62.2 31.9 %copy-start.5 = (f32[512,256]{0,1:T(8,128)}, f32[512,256]{0,1:T(8,128)S(1)}, u32[]{:S(2)}) copy-start(f32[512,256]{0,1:T(8,128)S(1)} %get-tuple-element.171) | copy-start | bytes 1572868
  62.3 29.1 %copy-start.14 = (bf16[2048,256]{1,0:T(8,128)(2,1)S(1)}, bf16[2048,256]{1,0:T(8,128)(2,1)}, u32[]{:S(2)}) copy-start(bf16[2048,256]{1,0:T(8,128)(2,1)} %param.16) | copy-start | bytes 3145732
  63.1 29.2 %copy-start.3 = (f32[512,256]{0,1:T(8,128)}, f32[512,256]{0,1:T(8,128)S(1)}, u32[]{:S(2)}) copy-start(f32[512,256]{0,1:T(8,128)S(1)} %fusion.159) | copy-start | bytes 1572868
  118.7 2.3 copy-start.1
  126.7 2.3 copy-start.1
  134.6 2.3 copy-start.1
  142.6 2.3 copy-start.1
  150.5 2.3 copy-start.1
  158.4 2.3 copy-start.1
  166.4 2.3 copy-start.1
  174.3 2.3 copy-start.1
  182.3 2.3 copy-start.1
  190.2 2.3 copy-start.1
  214.0 2.3 copy-start.1
  229.9 2.3 copy-start.1
  237.8 2.3 copy-start.1
  243.5 4.7 %copy-start.8 = (f32[512,256]{0,1:T(8,128)S(1)}, f32[512,256]{0,1:T(8,128)}, u32[]{:S(2)}) copy-start(f32[512,256]{0,1:T(8,128)} %copy-done.7) | copy-start | bytes 1572868
  243.5 30.4 %copy-start.6 = (f32[512,256]{0,1:T(8,128)S(1)}, f32[512,256]{0,1:T(8,128)}, u32[]{:S(2)}) copy-start(f32[512,256]{0,1:T(8,128)} %copy-done.5) | copy-start | bytes 1572868
  248.2 26.5 %copy-start.2 = (f32[2,512,512]{2,1,0:T(8,128)S(1)}, f32[2,512,512]{2,1,0:T(8,128)}, u32[]{:S(2)}) copy-start(f32[2,512,512]{2,1,0:T(8,128)} %exponential_multiply_fusion) | copy-start | bytes 6291460
  278.0 43.8 %all-to-all-start.1 = ((bf16[16,128,256]{1,2,0:T(8,128)(2,1)}), bf16[16,128,256]{1,2,0:T(8,128)(2,1)S(1)}, u32[]{:S(2)}, u32[]{:S(2)}) async-start(bf16[16,128,256]{1,2,0:T(8,128)(2,1)} %bitcast.304), calls=%async_computation.1 | async-start | bytes 2097152 | tf_op jit(solution)/shard_map/all_to_all | solution.py:105
  (9 other events, 16.5 us)
Sparse Core Ops, SparseCore 0:
  27.8 78.3 all-gather.6
where the time goes:
time: 333 us; the launch traced here: 331 us
  blocking collectives  133 us (40%)
  matrix products  70.3 us (21%)
  other arithmetic  43.5 us (13%)
  local copies, waits for them, and re-layouts  42.6 us (13%)
  between operations  16.8 us (5%)
  loops' own time  11.4 us (3%)
  waiting for transfers between devices  8.48 us (3%)
  starting transfers between devices  4.79 us (1%)
    psum x4, blocking collectives, by_axis(): value = lax.psum(value, axis)  37.5 us
    all_gather x3, blocking collectives, entering(): lax.all_gather(part.astype(kind), axis)  37.3 us
    reduce_sum x16, other arithmetic, attend(): row_total = row_total * factor + jnp.sum(weights, axis=2)  36.9 us
    all_gather x3, blocking collectives, carried_in(): lax.all_gather(part.astype(kind), axis)  31.8 us
    dot_general x16, matrix products, attend(): jnp.einsum('qhd,khd->hqk', queries, key_heads, preferred_element_type=jnp...  30.6 us
    dynamic_slice x32, local copies, waits for them, and re-layouts, fold_blocks(): return lax.scan(one_block, running, (block_ids, stacked))[0]  26.5 us
    dot_general x16, matrix products, attend(): jnp.einsum('hqk,khd->hqd', weights.astype(jnp.bfloat16), value_heads, pre...  17.6 us
    all_to_all x1, blocking collectives, copy_for_each(): lax.all_to_all(jnp.broadcast_to(value[None], (devices, *value.shape)), ax...  15.6 us
  transfers between devices with their start and end apart: 2, of which 1 were waited for; matrix products, arithmetic and copies ran while one was open for 5% of the time, Pallas kernels for 0%

commit v1 on v0

v1 whole, which is shorter than its diff:
```python
import math

import jax
import jax.numpy as jnp
from jax import lax
from jax.experimental import pallas as pl
from jax.experimental.pallas import tpu as pltpu
from jax.sharding import PartitionSpec as P

F32 = jnp.float32
BF16 = jnp.bfloat16
MESH = pl.DeviceIdType.MESH
NEG_FILL = -1e30
EPSILON = 1e-06

T = 512
D = 2048
HD = 128
NH = 2
W = NH * HD
LAT = 512
HALF = T // 2
ALL_TOKENS = 8192
ALL_HEADS = 16
EXP2_SCALE = math.log2(math.e) / math.sqrt(HD)

AWAY = (
    (0, -1), (-1, 0), (0, 1), (1, 0),
    (0, 2), (2, 0), (-1, -1), (1, -1), (-1, 1), (1, 1),
    (-1, 2), (1, 2), (2, -1), (2, 1),
    (2, 2),
)
LEVEL_AT = (0, 4, 10, 14)


def nt(a, b):
    return lax.dot_general(a, b, (((1,), (1,)), ((), ())), preferred_element_type=F32)


def nn(a, b):
    return jnp.dot(a, b, preferred_element_type=F32)


def tn(a, b):
    return lax.dot_general(a, b, (((0,), (0,)), ((), ())), preferred_element_type=F32)


def pick(index, values):
    out = jnp.int32(values[0])
    for k in range(1, len(values)):
        out = jnp.where(index == k, jnp.int32(values[k]), out)
    return out


def three_parts(a):
    hi = a.astype(BF16)
    rest = a - hi.astype(F32)
    mid = rest.astype(BF16)
    low = (rest - mid.astype(F32)).astype(BF16)
    return hi, mid, low


def kernel(
    tok_h, wl_h, wq_h, wku_h, wvu_h, wsq_h, wsk_h, wsv_h, fg_h,
    tout_ref, loss_ref, wg_ref,
    tok, tokt, wl, wall, wkv, fgv,
    lat, myp, pairin, pairbuf, kbuf, vbuf, qbuf, acc, mrun,
    sq, sk, sv, ccol, crow, mix, sout, startq, endk, vg,
    sx, sy, mx, my, bx, by, lx, ly, lz, lc,
    pw, r1in, r1own, r2in,
    load_sem, pair_s, pair_r, z_s, z_r, gs, gr, ds_, dr,
    st_s, st_r, rs_s, rs_r, ls_s, ls_r,
):
    s = lax.axis_index("seq")
    t = lax.axis_index("tensor")
    y, x = s // 4, s % 4
    z, c = t // 2, t % 2
    hb = c * HALF

    def plane(yy, xx):
        return (yy * 4 + xx, t)

    def x_peer(d):
        return plane(y, (x + d) % 4)

    def y_peer(d):
        return plane((y + d) % 4, x)

    def z_peer(d):
        return (s, ((z + d) % 4) * 2 + c)

    partner = (s, z * 2 + (1 - c))

    def remote(src, dst, send, recv, to):
        return pltpu.make_async_remote_copy(
            src_ref=src, dst_ref=dst, send_sem=send, recv_sem=recv, device_id=to, device_id_type=MESH
        )

    wl[...] = jnp.zeros_like(wl)
    loads = [
        pltpu.make_async_copy(wl_h, wl.at[pl.ds(pl.multiple_of(c * 64, 64), 64), :], load_sem.at[0]),
        pltpu.make_async_copy(tok_h, tok, load_sem.at[1]),
        pltpu.make_async_copy(wq_h, wall.at[0], load_sem.at[2]),
        pltpu.make_async_copy(wsk_h, wall.at[1], load_sem.at[3]),
        pltpu.make_async_copy(wsv_h, wall.at[2], load_sem.at[4]),
        pltpu.make_async_copy(wsq_h, wall.at[3], load_sem.at[5]),
        pltpu.make_async_copy(fg_h, fgv, load_sem.at[6]),
        pltpu.make_async_copy(wku_h, wkv.at[:, 0:W], load_sem.at[7]),
        pltpu.make_async_copy(wvu_h, wkv.at[:, W : 2 * W], load_sem.at[8]),
    ]
    for copy in loads:
        copy.start()
    barrier = pltpu.get_barrier_semaphore()
    peers = [x_peer(d) for d in (1, 2, 3)] + [y_peer(d) for d in (1, 2, 3)]
    peers += [z_peer(d) for d in (1, 2, 3)] + [partner]
    for peer in peers:
        pl.semaphore_signal(barrier, inc=1, device_id=peer, device_id_type=MESH)

    loads[0].wait()
    loads[1].wait()
    myp[...] = nt(tok[...], wl[...]).astype(BF16)
    pl.semaphore_wait(barrier, 10)
    other = pl.multiple_of((1 - c) * HALF, HALF)
    own = pl.multiple_of(hb, HALF)
    to_pair = remote(myp.at[pl.ds(other, HALF), :], pairin, pair_s, pair_r, partner)
    to_pair.start()

    def project(i):
        return nn(tok[...], wall[i])

    loads[2].wait()
    qbuf[...] = project(0).astype(BF16)
    to_pair.wait_recv()
    pairbuf[...] = myp[pl.ds(own, HALF), :] + pairin[...]
    my_slice = lat.at[y, x, z, pl.ds(own, HALF), :]
    to_z = [remote(pairbuf, my_slice, z_s.at[d - 1], z_r.at[d - 1], z_peer(d)) for d in (1, 2, 3)]
    for copy in to_z:
        copy.start()
    lat[y, x, z, pl.ds(own, HALF), :] = pairbuf[...]

    def unit(h, m):
        part = m[:, h * HD : (h + 1) * HD]
        return part * lax.rsqrt(jnp.sum(part * part, axis=-1, keepdims=True) + EPSILON)

    loads[6].wait()
    row_at = lax.broadcasted_iota(jnp.int32, (T, T), 0)
    col_at = lax.broadcasted_iota(jnp.int32, (T, T), 1)
    lower = (col_at <= row_at).astype(BF16)
    f_parts = three_parts(fgv[...])
    crow[0:NH, :] = sum(nt(part, lower) for part in f_parts)
    for h in range(NH):
        spread = [jnp.broadcast_to(part[h : h + 1, :], (HD, T)) for part in f_parts]
        ccol[h] = sum(nt(lower, part) for part in spread)

    loads[3].wait()
    keys_f = project(1)
    loads[4].wait()
    sv[...] = project(2).astype(BF16)
    ends = []
    for h in range(NH):
        cols = slice(h * HD, (h + 1) * HD)
        unit_k = unit(h, keys_f)
        sk[:, cols] = unit_k.astype(BF16)
        end_row = ccol[h, T - 1 : T, :]
        endk[:, cols] = (unit_k * jnp.exp(end_row - ccol[h])).astype(BF16)
        ends.append(end_row)
    blank = jnp.zeros((8 - NH, HD), F32)
    mx[x] = jnp.concatenate(ends + [blank], axis=0)
    for h in range(NH):
        cols = slice(h * HD, (h + 1) * HD)
        sx[x, cols, :] = tn(endk[:, cols], sv[:, cols]).astype(BF16)

    def row_sends(buf, sems, first, peer_of, slot):
        return [
            remote(buf.at[slot], buf.at[slot], sems[0].at[first + d - 1], sems[1].at[first + d - 1], peer_of(d))
            for d in (1, 2, 3)
        ]

    st = (st_s, st_r)
    fwd_x = row_sends(sx, st, 0, x_peer, x) + row_sends(mx, st, 3, x_peer, x)
    for copy in fwd_x:
        copy.start()

    loads[5].wait()
    queries_f = project(3)
    for h in range(NH):
        cols = slice(h * HD, (h + 1) * HD)
        unit_q = unit(h, queries_f)
        sq[:, cols] = unit_q.astype(BF16)
        startq[:, cols] = (unit_q * jnp.exp(ccol[h])).astype(BF16)

    def piece(idx, yy, xx, lo, size, to):
        ref = lat.at[yy % 4, xx % 4, :, pl.ds(pl.multiple_of(hb + lo, 64), size), :]
        return remote(ref, ref, gs.at[idx], gr.at[idx], to)

    xp, xm, yp, ym = x_peer(1), x_peer(3), y_peer(1), y_peer(3)
    level_1 = [
        piece(0, y, x, 0, HALF, xp),
        piece(1, y, x, 0, HALF, xm),
        piece(2, y, x, 0, HALF, yp),
        piece(3, y, x, 0, HALF, ym),
    ]
    level_2 = [
        piece(4, y, x - 1, 0, 128, xp),
        piece(5, y, x + 1, 128, 128, xm),
        piece(6, y - 1, x, 0, 128, yp),
        piece(7, y + 1, x, 128, 128, ym),
        piece(8, y, x - 1, 0, 128, yp),
        piece(9, y, x - 1, 0, 128, ym),
        piece(10, y, x + 1, 0, 128, yp),
        piece(11, y, x + 1, 0, 128, ym),
        piece(12, y - 1, x, 128, 128, xp),
        piece(13, y - 1, x, 128, 128, xm),
        piece(14, y + 1, x, 128, 128, xp),
        piece(15, y + 1, x, 128, 128, xm),
    ]
    level_3 = [
        piece(16, y, x + 2, 0, 128, yp),
        piece(17, y, x + 2, 0, 128, ym),
        piece(18, y + 2, x, 128, 128, xp),
        piece(19, y + 2, x, 128, 128, xm),
        piece(20, y - 1, x - 1, 0, 64, yp),
        piece(21, y + 1, x - 1, 64, 64, ym),
        piece(22, y - 1, x + 1, 0, 64, yp),
        piece(23, y + 1, x + 1, 64, 64, ym),
        piece(24, y - 1, x - 1, 128, 64, xp),
        piece(25, y - 1, x + 1, 192, 64, xm),
        piece(26, y + 1, x - 1, 128, 64, xp),
        piece(27, y + 1, x + 1, 192, 64, xm),
    ]
    level_4 = [
        piece(28, y - 1, x + 2, 0, 64, yp),
        piece(29, y + 1, x + 2, 64, 64, ym),
        piece(30, y + 2, x - 1, 128, 64, xp),
        piece(31, y + 2, x + 1, 192, 64, xm),
    ]
    levels = (level_1, level_2, level_3, level_4)

    def to_partner(i, yy, xx):
        ref = lat.at[yy, xx, :, pl.ds(own, HALF), :]
        return remote(ref, ref, ds_.at[i], dr.at[i], partner)

    def away(i):
        return (y + AWAY[i][0]) % 4, (x + AWAY[i][1]) % 4

    for copy in to_z:
        copy.wait_recv()
    for copy in level_1:
        copy.start()
    own_to_partner = to_partner(15, y, x)
    own_to_partner.start()

    for h in range(NH):
        cols = slice(h * HD, (h + 1) * HD)
        raw = nt(sq[:, cols], sk[:, cols])
        gaps = ccol[h, :, 0:1] - crow[h : h + 1, :]
        mix[h] = (raw * jnp.exp(jnp.where(col_at <= row_at, gaps, NEG_FILL))).astype(BF16)
    for h in range(NH):
        cols = slice(h * HD, (h + 1) * HD)
        sout[:, cols] = nn(mix[h], sv[:, cols])

    for copy in fwd_x:
        copy.wait_recv()

    def stage(buf, decays, position, order, h):
        rows = slice(h * HD, (h + 1) * HD)
        running = jnp.zeros((HD, HD), F32)
        total = jnp.zeros((1, HD), F32)
        inside, inside_log = running, total
        for k in order:
            here = position == k
            inside = jnp.where(here, running, inside)
            inside_log = jnp.where(here, total, inside_log)
            log_decay = decays[k, h : h + 1, :]
            running = running * jnp.exp(log_decay) + buf[k, rows, :].astype(F32)
            total = total + log_decay
        return inside, inside_log, running, total

    rise, fall = (0, 1, 2, 3), (3, 2, 1, 0)
    row_inside, ends = [], []
    for h in range(NH):
        inside, inside_log, running, total = stage(sx, mx, x, rise, h)
        row_inside.append((inside, inside_log))
        sy[y, h * HD : (h + 1) * HD, :] = running.astype(BF16)
        ends.append(total)
    my[y] = jnp.concatenate(ends + [blank], axis=0)
    fwd_y = row_sends(sy, st, 6, y_peer, y) + row_sends(my, st, 9, y_peer, y)
    for copy in fwd_y:
        copy.start()

    def tok_turn(i, carry):
        cut = pl.ds(pl.multiple_of(i * 256, 256), 256)
        tokt[cut, :] = jnp.transpose(tok[:, cut])
        return carry

    lax.fori_loop(0, D // 256, tok_turn, 0)

    for h in range(NH):
        vbuf[h, :, HD:W] = jnp.ones((T, HD), BF16)
    loads[7].wait()
    loads[8].wait()

    def up(yy, xx):
        block = jnp.concatenate([lat[yy, xx, k] for k in range(4)], axis=1)
        kbuf[...] = nn(block, wkv[:, 0:W]).astype(BF16)
        values = nn(block, wkv[:, W : 2 * W]).astype(BF16)
        for h in range(NH):
            vbuf[h, :, 0:HD] = values[:, h * HD : (h + 1) * HD]

    own_to_partner.wait_recv()
    up(y, x)
    for h in range(NH):
        cols = slice(h * HD, (h + 1) * HD)
        for part in range(4):
            rows = slice(part * 128, (part + 1) * 128)
            upto = (part + 1) * 128
            scores = nt(qbuf[rows, cols], kbuf[0:upto, cols])
            r = lax.broadcasted_iota(jnp.int32, (128, upto), 0) + part * 128
            k = lax.broadcasted_iota(jnp.int32, (128, upto), 1)
            scores = jnp.where(k <= r, scores, NEG_FILL)
            best = jnp.max(scores, axis=1, keepdims=True)
            weights = jnp.exp2((scores - best) * EXP2_SCALE).astype(BF16)
            acc[h, rows, :] = nn(weights, vbuf[h, 0:upto, :])
            mrun[h, rows, :] = jnp.broadcast_to(best, (128, HD))

    def block_step(i, carry):
        for n, first in enumerate(LEVEL_AT):

            @pl.when(i == first)
            def _():
                for copy in levels[n]:
                    copy.wait_recv()
                if n < 3:
                    for copy in levels[n + 1]:
                        copy.start()
                last = LEVEL_AT[n + 1] if n < 3 else 15
                for b in range(first, last):
                    to_partner(b, *away(b)).start()

        yy = (y + pick(i, [a[0] for a in AWAY]) + 4) % 4
        xx = (x + pick(i, [a[1] for a in AWAY]) + 4) % 4
        to_partner(i, yy, xx).wait_recv()

        @pl.when(yy * 4 + xx < s)
        def _():
            up(yy, xx)
            for h in range(NH):
                cols = slice(h * HD, (h + 1) * HD)
                for part in range(4):
                    rows = slice(part * 128, (part + 1) * 128)
                    scores = nt(qbuf[rows, cols], kbuf[:, cols])
                    old = mrun[h, rows, :]
                    best = jnp.maximum(old, jnp.max(scores, axis=1, keepdims=True))
                    weights = jnp.exp2((scores - best[:, 0:1]) * EXP2_SCALE).astype(BF16)
                    factor = jnp.exp2((old - best) * EXP2_SCALE)
                    both = jnp.concatenate([factor, factor], axis=1)
                    acc[h, rows, :] = acc[h, rows, :] * both + nn(weights, vbuf[h])
                    mrun[h, rows, :] = best

        return carry

    lax.fori_loop(0, 15, block_step, 0)

    for copy in fwd_y:
        copy.wait_recv()
    for h in range(NH):
        cols = slice(h * HD, (h + 1) * HD)
        inside_y = stage(sy, my, y, rise, h)[0]
        inside, inside_log = row_inside[h]
        prefix = (inside + jnp.exp(inside_log) * inside_y).astype(BF16)
        sout[:, cols] = sout[:, cols] + nn(startq[:, cols], prefix)

    squares = jnp.zeros((8, HD), F32)
    inv = 1.0 / math.sqrt(ALL_TOKENS)
    for h in range(NH):
        cols = slice(h * HD, (h + 1) * HD)
        teacher = (acc[h, :, 0:HD] / acc[h, :, HD:W]).astype(BF16)
        tout_ref[:, cols] = teacher
        mismatch = sout[:, cols] - teacher.astype(F32)
        squares += jnp.sum((mismatch * mismatch).reshape(T // 8, 8, HD), axis=0)
        vg[:, cols] = (mismatch * inv).astype(BF16)
    for h in range(NH):
        cols = slice(h * HD, (h + 1) * HD)
        bx[x, cols, :] = tn(startq[:, cols], vg[:, cols]).astype(BF16)
    lx[x] = squares
    ls = (ls_s, ls_r)
    back_x = row_sends(bx, st, 12, x_peer, x)
    loss_x = row_sends(lx, ls, 0, x_peer, x)
    for copy in back_x + loss_x:
        copy.start()
    for h in range(NH):
        cols = slice(h * HD, (h + 1) * HD)
        sout[:, cols] = tn(mix[h], vg[:, cols])

    for copy in back_x:
        copy.wait_recv()
    row_inside = []
    for h in range(NH):
        inside, inside_log, running, _ = stage(bx, mx, x, fall, h)
        row_inside.append((inside, inside_log))
        by[y, h * HD : (h + 1) * HD, :] = running.astype(BF16)
    back_y = row_sends(by, st, 15, y_peer, y)
    for copy in back_y:
        copy.start()
    for copy in loss_x:
        copy.wait_recv()
    ly[y] = lx[0] + lx[1] + lx[2] + lx[3]
    loss_y = row_sends(ly, ls, 3, y_peer, y)
    for copy in loss_y:
        copy.start()
    for copy in back_y:
        copy.wait_recv()
    for h in range(NH):
        cols = slice(h * HD, (h + 1) * HD)
        inside_y = stage(by, my, y, fall, h)[0]
        inside, inside_log = row_inside[h]
        suffix = (inside + jnp.exp(inside_log) * inside_y).astype(BF16)
        vg[:, cols] = (sout[:, cols] + nn(endk[:, cols], suffix)).astype(BF16)

    def wgrad(i, carry):
        part = nn(tokt[pl.ds(pl.multiple_of(i * 512, 512), 512), :], vg[...]).astype(BF16)
        for k in range(4):
            for h in range(NH):
                pw[h, i, k] = part[k * 128 : (k + 1) * 128, h * HD : (h + 1) * HD]
        return carry

    lax.fori_loop(0, 4, wgrad, 0)
    rs_x1 = [
        remote(pw.at[0, :, (x + d) % 4], r1in.at[0, d - 1], rs_s.at[d - 1], rs_r.at[d - 1], x_peer(d))
        for d in (1, 2, 3)
    ]
    rs_y1 = [
        remote(pw.at[1, (y + d) % 4], r1in.at[1, d - 1], rs_s.at[d + 2], rs_r.at[d + 2], y_peer(d))
        for d in (1, 2, 3)
    ]
    for copy in rs_x1 + rs_y1:
        copy.start()
    for copy in loss_y:
        copy.wait_recv()
    lz[z] = ly[0] + ly[1] + ly[2] + ly[3]
    loss_z = row_sends(lz, ls, 6, z_peer, z)
    for copy in loss_z:
        copy.start()

    for copy in rs_x1:
        copy.wait_recv()
    mine = [pw[0, k, x].astype(F32) for k in range(4)]
    for k in range(4):
        r1own[0, k] = (mine[k] + sum(r1in[0, d, k].astype(F32) for d in range(3))).astype(BF16)
    rs_y2 = [
        remote(r1own.at[0, (y + d) % 4], r2in.at[0, d - 1], rs_s.at[d + 5], rs_r.at[d + 5], y_peer(d))
        for d in (1, 2, 3)
    ]
    for copy in rs_y2:
        copy.start()
    for copy in rs_y1:
        copy.wait_recv()
    mine = [pw[1, y, k].astype(F32) for k in range(4)]
    for k in range(4):
        r1own[1, k] = (mine[k] + sum(r1in[1, d, k].astype(F32) for d in range(3))).astype(BF16)
    rs_x2 = [
        remote(r1own.at[1, (x + d) % 4], r2in.at[1, d - 1], rs_s.at[d + 8], rs_r.at[d + 8], x_peer(d))
        for d in (1, 2, 3)
    ]
    for copy in rs_x2:
        copy.start()

    for copy in loss_z:
        copy.wait_recv()
    lc[c] = lz[0] + lz[1] + lz[2] + lz[3]
    loss_c = remote(lc.at[c], lc.at[c], ls_s.at[9], ls_r.at[9], partner)
    loss_c.start()
    loss_c.wait_recv()
    loss_ref[0, 0] = jnp.sum(lc[0] + lc[1]) / (2.0 * ALL_TOKENS * ALL_HEADS * HD)

    for copy in rs_y2:
        copy.wait_recv()
    wg_ref[:, 0:HD] = r1own[0, y].astype(F32) + sum(r2in[0, d].astype(F32) for d in range(3))
    for copy in rs_x2:
        copy.wait_recv()
    wg_ref[:, HD:W] = r1own[1, x].astype(F32) + sum(r2in[1, d].astype(F32) for d in range(3))

    sent = [to_pair] + to_z + fwd_x + fwd_y + back_x + back_y
    sent += loss_x + loss_y + loss_z + [loss_c] + rs_x1 + rs_y1 + rs_y2 + rs_x2
    for level in levels:
        sent += level
    sent += [to_partner(b, *away(b)) for b in range(15)] + [own_to_partner]
    for copy in sent:
        copy.wait_send()


def per_device(tokens, w_latent, w_query, w_key_up, w_value_up, w_stu_query, w_stu_key, w_stu_value, forget):
    dma = pltpu.SemaphoreType.DMA
    scratch = [
        pltpu.VMEM((T, D), BF16),
        pltpu.VMEM((D, T), BF16),
        pltpu.VMEM((HD, D), BF16),
        pltpu.VMEM((4, D, W), BF16),
        pltpu.VMEM((LAT, 2 * W), BF16),
        pltpu.VMEM((NH, T), F32),
        pltpu.VMEM((4, 4, 4, T, HD), BF16),
        pltpu.VMEM((T, HD), BF16),
        pltpu.VMEM((HALF, HD), BF16),
        pltpu.VMEM((HALF, HD), BF16),
        pltpu.VMEM((T, W), BF16),
        pltpu.VMEM((NH, T, W), BF16),
        pltpu.VMEM((T, W), BF16),
        pltpu.VMEM((NH, T, W), F32),
        pltpu.VMEM((NH, T, HD), F32),
        pltpu.VMEM((T, W), BF16),
        pltpu.VMEM((T, W), BF16),
        pltpu.VMEM((T, W), BF16),
        pltpu.VMEM((NH, T, HD), F32),
        pltpu.VMEM((8, T), F32),
        pltpu.VMEM((NH, T, T), BF16),
        pltpu.VMEM((T, W), F32),
        pltpu.VMEM((T, W), BF16),
        pltpu.VMEM((T, W), BF16),
        pltpu.VMEM((T, W), BF16),
        pltpu.VMEM((4, W, HD), BF16),
        pltpu.VMEM((4, W, HD), BF16),
        pltpu.VMEM((4, 8, HD), F32),
        pltpu.VMEM((4, 8, HD), F32),
        pltpu.VMEM((4, W, HD), BF16),
        pltpu.VMEM((4, W, HD), BF16),
        pltpu.VMEM((4, 8, HD), F32),
        pltpu.VMEM((4, 8, HD), F32),
        pltpu.VMEM((4, 8, HD), F32),
        pltpu.VMEM((2, 8, HD), F32),
        pltpu.VMEM((NH, 4, 4, 128, HD), BF16),
        pltpu.VMEM((NH, 3, 4, 128, HD), BF16),
        pltpu.VMEM((NH, 4, 128, HD), BF16),
        pltpu.VMEM((NH, 3, 128, HD), BF16),
        dma((9,)),
        dma,
        dma,
        dma((3,)),
        dma((3,)),
        dma((32,)),
        dma((32,)),
        dma((16,)),
        dma((16,)),
        dma((18,)),
        dma((18,)),
        dma((12,)),
        dma((12,)),
        dma((10,)),
        dma((10,)),
    ]
    anywhere = pl.BlockSpec(memory_space=pl.ANY)
    teacher, loss, wgrad = pl.pallas_call(
        kernel,
        out_shape=(
            jax.ShapeDtypeStruct((T, W), BF16),
            jax.ShapeDtypeStruct((1, 1), F32),
            jax.ShapeDtypeStruct((128, W), F32),
        ),
        in_specs=[anywhere] * 9,
        out_specs=(
            pl.BlockSpec(memory_space=pltpu.VMEM),
            pl.BlockSpec(memory_space=pltpu.SMEM),
            pl.BlockSpec(memory_space=pltpu.VMEM),
        ),
        scratch_shapes=scratch,
        compiler_params=pltpu.CompilerParams(
            collective_id=0, has_side_effects=True, vmem_limit_bytes=60 * 1024 * 1024
        ),
    )(
        tokens, w_latent.T, w_query, w_key_up, w_value_up, w_stu_query, w_stu_key, w_stu_value, forget.T
    )
    return teacher, loss[0, 0], wgrad


def solution(mesh):
    return jax.shard_map(
        per_device,
        mesh=mesh,
        in_specs=(
            P("seq", None),
            P(None, "tensor"),
            P(None, "tensor"),
            P(None, "tensor"),
            P(None, "tensor"),
            P(None, "tensor"),
            P(None, "tensor"),
            P(None, "tensor"),
            P("seq", "tensor"),
        ),
        out_specs=(P("seq", "tensor"), P(), P("seq", "tensor")),
        check_vma=False,
    )
```

time: 333 us -> 96.6 us (0.29)
  blocking collectives: 133 us -> 0 us
  Pallas kernels: 0 us -> 90.8 us
  matrix products: 70.3 us -> 0 us
  other arithmetic: 43.5 us -> 0 us
  local copies, waits for them, and re-layouts: 42.6 us -> 3.24 us
  between operations: 16.8 us -> 2.4 us
  loops' own time: 11.4 us -> 0 us
  waiting for transfers between devices: 8.48 us -> 0 us
  starting transfers between devices: 4.79 us -> 0 us
    pallas_call x0 -> x1, Pallas kernels: none -> 90.8 us  [per_device(): pl.pallas_call(kernel, out_shape=(jax.ShapeDtypeStruct((T, W), BF16), jax...]
    dot_general x47 -> x0, matrix products: 70.3 us -> none  [the longest x16 30.6 us: attend(): jnp.einsum('qhd,khd->hqk', queries, key_heads, preferred_element_type=jnp...]
    all_gather x6 -> x0, blocking collectives: 69.2 us -> none  [the longest x3 37.3 us: entering(): lax.all_gather(part.astype(kind), axis)]
    psum x4 -> x0, blocking collectives: 37.5 us -> none  [by_axis(): value = lax.psum(value, axis)]
    reduce_sum x17 -> x0, other arithmetic: 37 us -> none  [the longest x16 36.9 us: attend(): row_total = row_total * factor + jnp.sum(weights, axis=2)]
    dynamic_slice x32 -> x0, local copies, waits for them, and re-layouts: 26.5 us -> none  [fold_blocks(): return lax.scan(one_block, running, (block_ids, stacked))[0]]
    all_to_all x1 -> x0, blocking collectives: 15.6 us -> none  [copy_for_each(): lax.all_to_all(jnp.broadcast_to(value[None], (devices, *value.shape)), ax...]
    another operation x1 -> x0, loops' own time: 11.4 us -> none  [fold_blocks(): return lax.scan(one_block, running, (block_ids, stacked))[0]]
  transfers between devices with their start and end apart: 2 -> 0, of which waited for: 1 -> 0; matrix products, arithmetic and copies ran while one was open for 5% -> 0% of each run, Pallas kernels for 0% -> 0%
where the time goes in v1:
time: 96.6 us; the launch traced here: 96.4 us
  Pallas kernels  90.8 us (94%)
  local copies, waits for them, and re-layouts  3.24 us (3%)
  between operations  2.4 us (2%)
    pallas_call x1, Pallas kernels, per_device(): pl.pallas_call(kernel, out_shape=(jax.ShapeDtypeStruct((T, W), BF16), jax...  90.8 us
    unnamed x2, local copies, waits for them, and re-layouts  3.24 us

profile of v1, /device:TPU:0, one launch (start us, length us, event | category | flops | bytes accessed | tf_op | source)
XLA Modules:
  0.0 96.4 jit_solution(6956508051877265437)
XLA Ops:
  0.6 90.8 %shard_map.112 = (bf16[512,256]{1,0:T(8,128)(2,1)}, f32[1,1]{1,0:T(1,128)}, f32[128,256]{1,0:T(8,128)}) custom-call(bf16[512,2048]{1,0:T(8,128)(2,1)} %tok_h.1, bf16[64,2048]{1,0:T(8,128)(2,1)} %bitcast.3, bf16[2048,256]{1,0:T(8,128)(2,1)} %wq_h.1, bf16[512,256]{1,0:T(8,128)(2,1)} %wku_h.1, bf16[512,256]{1,0:T(8,128)(2,1)} %wvu_h.1, ...), custom_call_target="tpu_custom_call" | custom-call | tf_op jit(solution)/shard_map/pallas_call | solution.py:551
  91.4 1.7 %copy.15 = bf16[512,256]{1,0:T(8,128)(2,1)} copy(bf16[512,256]{1,0:T(8,128)(2,1)} %get-tuple-element.12) | data formatting | bytes 524288
  93.7 1.6 %copy.17 = f32[128,256]{1,0:T(8,128)} copy(f32[128,256]{1,0:T(8,128)} %get-tuple-element.14) | data formatting | bytes 262144

commit v2 on v1

--- a/solution.py
+++ b/solution.py
@@ -20,17 +20,19 @@
 W = NH * HD
 LAT = 512
 HALF = T // 2
+ONES = 16
 ALL_TOKENS = 8192
 ALL_HEADS = 16
 EXP2_SCALE = math.log2(math.e) / math.sqrt(HD)
 
 AWAY = (
-    (0, -1), (-1, 0), (0, 1), (1, 0),
-    (0, 2), (2, 0), (-1, -1), (1, -1), (-1, 1), (1, 1),
+    (-1, 0), (1, 0), (0, -1), (0, 1),
+    (2, 0), (-1, -1), (1, -1), (-1, 1), (1, 1), (0, 2),
     (-1, 2), (1, 2), (2, -1), (2, 1),
     (2, 2),
 )
-LEVEL_AT = (0, 4, 10, 14)
+LEVEL_BLOCKS = ((0, 4), (4, 10), (10, 14), (14, 15))
+LEVEL_STEP = (None, 0, 2, 3)
 
 
 def nt(a, b):
@@ -63,12 +65,12 @@
 def kernel(
     tok_h, wl_h, wq_h, wku_h, wvu_h, wsq_h, wsk_h, wsv_h, fg_h,
     tout_ref, loss_ref, wg_ref,
-    tok, tokt, wl, wall, wkv, fgv,
-    lat, myp, pairin, pairbuf, kbuf, vbuf, qbuf, acc, mrun,
+    tok, tokt, wl, wall, wk, wv, wvt, fgv,
+    lat, myp, pairin, pairbuf, kbuf, vt, qbuf, acc, mrun,
     sq, sk, sv, ccol, crow, mix, sout, startq, endk, vg,
-    sx, sy, mx, my, bx, by, lx, ly, lz, lc,
+    held, heldlog, sx, sy, mx, my, bx, by, lx, ly, lz, lc,
     pw, r1in, r1own, r2in,
-    load_sem, pair_s, pair_r, z_s, z_r, gs, gr, ds_, dr,
+    load_sem, pair_s, pair_r, z_s, z_r, gs, gr, zg_s, zg_r, ds_, dr,
     st_s, st_r, rs_s, rs_r, ls_s, ls_r,
 ):
     s = lax.axis_index("seq")
@@ -105,11 +107,13 @@
         pltpu.make_async_copy(wsv_h, wall.at[2], load_sem.at[4]),
         pltpu.make_async_copy(wsq_h, wall.at[3], load_sem.at[5]),
         pltpu.make_async_copy(fg_h, fgv, load_sem.at[6]),
-        pltpu.make_async_copy(wku_h, wkv.at[:, 0:W], load_sem.at[7]),
-        pltpu.make_async_copy(wvu_h, wkv.at[:, W : 2 * W], load_sem.at[8]),
-    ]
-    for copy in loads:
-        copy.start()
+    ]
+    for j in range(4):
+        rows = pl.ds(pl.multiple_of((z + j) % 4 * HD, HD), HD)
+        loads.append(pltpu.make_async_copy(wku_h.at[rows, :], wk.at[j * HD : (j + 1) * HD, :], load_sem.at[7 + j]))
+        loads.append(pltpu.make_async_copy(wvu_h.at[rows, :], wv.at[j * HD : (j + 1) * HD, :], load_sem.at[11 + j]))
+    loads[0].start()
+    loads[1].start()
     barrier = pltpu.get_barrier_semaphore()
     peers = [x_peer(d) for d in (1, 2, 3)] + [y_peer(d) for d in (1, 2, 3)]
     peers += [z_peer(d) for d in (1, 2, 3)] + [partner]
@@ -118,6 +122,8 @@
 
     loads[0].wait()
     loads[1].wait()
+    for copy in loads[2:]:
+        copy.start()
     myp[...] = nt(tok[...], wl[...]).astype(BF16)
     pl.semaphore_wait(barrier, 10)
     other = pl.multiple_of((1 - c) * HALF, HALF)
@@ -133,10 +139,27 @@
     to_pair.wait_recv()
     pairbuf[...] = myp[pl.ds(own, HALF), :] + pairin[...]
     my_slice = lat.at[y, x, z, pl.ds(own, HALF), :]
-    to_z = [remote(pairbuf, my_slice, z_s.at[d - 1], z_r.at[d - 1], z_peer(d)) for d in (1, 2, 3)]
-    for copy in to_z:
-        copy.start()
-    lat[y, x, z, pl.ds(own, HALF), :] = pairbuf[...]
+    lat[y, x, 0, pl.ds(own, HALF), :] = pairbuf[...]
+
+    def slot(yy, xx, j):
+        return lat.at[yy, xx, j, pl.ds(own, HALF), :]
+
+    to_z = [
+        remote(pairbuf, slot(y, x, 4 - d), z_s.at[d - 1], z_r.at[d - 1], z_peer(d)) for d in (1, 2, 3)
+    ]
+    for d in (3, 1, 2):
+        to_z[d - 1].start()
+    xp, xm, yp, ym = x_peer(1), x_peer(3), y_peer(1), y_peer(3)
+
+    def near(j):
+        return [
+            remote(slot(y, x, j), slot(y, x, j), gs.at[32 + 2 * k + j], gr.at[32 + 2 * k + j], to)
+            for k, to in enumerate((yp, ym, xp, xm))
+        ]
+
+    level_1 = [near(0), near(1)]
+    for copy in level_1[0]:
+        copy.start()
 
     def unit(h, m):
         part = m[:, h * HD : (h + 1) * HD]
@@ -156,6 +179,9 @@
     keys_f = project(1)
     loads[4].wait()
     sv[...] = project(2).astype(BF16)
+    to_z[2].wait_recv()
+    for copy in level_1[1]:
+        copy.start()
     ends = []
     for h in range(NH):
         cols = slice(h * HD, (h + 1) * HD)
@@ -178,9 +204,6 @@
 
     st = (st_s, st_r)
     fwd_x = row_sends(sx, st, 0, x_peer, x) + row_sends(mx, st, 3, x_peer, x)
-    for copy in fwd_x:
-        copy.start()
-
     loads[5].wait()
     queries_f = project(3)
     for h in range(NH):
@@ -190,16 +213,9 @@
         startq[:, cols] = (unit_q * jnp.exp(ccol[h])).astype(BF16)
 
     def piece(idx, yy, xx, lo, size, to):
-        ref = lat.at[yy % 4, xx % 4, :, pl.ds(pl.multiple_of(hb + lo, 64), size), :]
+        ref = lat.at[yy % 4, xx % 4, 0:2, pl.ds(pl.multiple_of(hb + lo, 64), size), :]
         return remote(ref, ref, gs.at[idx], gr.at[idx], to)
 
-    xp, xm, yp, ym = x_peer(1), x_peer(3), y_peer(1), y_peer(3)
-    level_1 = [
-        piece(0, y, x, 0, HALF, xp),
-        piece(1, y, x, 0, HALF, xm),
-        piece(2, y, x, 0, HALF, yp),
-        piece(3, y, x, 0, HALF, ym),
-    ]
     level_2 = [
         piece(4, y, x - 1, 0, 128, xp),
         piece(5, y, x + 1, 128, 128, xm),
@@ -234,21 +250,36 @@
         piece(30, y + 2, x - 1, 128, 64, xp),
         piece(31, y + 2, x + 1, 192, 64, xm),
     ]
-    levels = (level_1, level_2, level_3, level_4)
+    levels = (sum(level_1, []), level_2, level_3, level_4)
 
     def to_partner(i, yy, xx):
         ref = lat.at[yy, xx, :, pl.ds(own, HALF), :]
         return remote(ref, ref, ds_.at[i], dr.at[i], partner)
 
+    def other_slices(b, yy, xx):
+        return (
+            remote(slot(yy, xx, 0), slot(yy, xx, 3), zg_s.at[2 * b], zg_r.at[2 * b], z_peer(1)),
+            remote(slot(yy, xx, 1), slot(yy, xx, 2), zg_s.at[2 * b + 1], zg_r.at[2 * b + 1], z_peer(3)),
+        )
+
+    def arrive(n):
+        for copy in levels[n]:
+            copy.wait_recv()
+        if n < 3:
+            for copy in levels[n + 1]:
+                copy.start()
+        for b in range(*LEVEL_BLOCKS[n]):
+            for copy in other_slices(b, *away(b)):
+                copy.start()
+
     def away(i):
         return (y + AWAY[i][0]) % 4, (x + AWAY[i][1]) % 4
 
-    for copy in to_z:
-        copy.wait_recv()
-    for copy in level_1:
-        copy.start()
+    to_z[0].wait_recv()
+    to_z[1].wait_recv()
     own_to_partner = to_partner(15, y, x)
     own_to_partner.start()
+    arrive(0)
 
     for h in range(NH):
         cols = slice(h * HD, (h + 1) * HD)
@@ -258,9 +289,6 @@
     for h in range(NH):
         cols = slice(h * HD, (h + 1) * HD)
         sout[:, cols] = nn(mix[h], sv[:, cols])
-
-    for copy in fwd_x:
-        copy.wait_recv()
 
     def stage(buf, decays, position, order, h):
         rows = slice(h * HD, (h + 1) * HD)
@@ -277,16 +305,22 @@
         return inside, inside_log, running, total
 
     rise, fall = (0, 1, 2, 3), (3, 2, 1, 0)
-    row_inside, ends = [], []
-    for h in range(NH):
-        inside, inside_log, running, total = stage(sx, mx, x, rise, h)
-        row_inside.append((inside, inside_log))
-        sy[y, h * HD : (h + 1) * HD, :] = running.astype(BF16)
-        ends.append(total)
-    my[y] = jnp.concatenate(ends + [blank], axis=0)
     fwd_y = row_sends(sy, st, 6, y_peer, y) + row_sends(my, st, 9, y_peer, y)
-    for copy in fwd_y:
-        copy.start()
+
+    def forward_row():
+        for copy in fwd_x:
+            copy.wait_recv()
+        ends = []
+        for h in range(NH):
+            rows = slice(h * HD, (h + 1) * HD)
+            inside, inside_log, running, total = stage(sx, mx, x, rise, h)
+            held[rows, :] = inside
+            heldlog[h : h + 1, :] = inside_log
+            sy[y, rows, :] = running.astype(BF16)
+            ends.append(total)
+        my[y] = jnp.concatenate(ends + [blank], axis=0)
+        for copy in fwd_y:
+            copy.start()
 
     def tok_turn(i, carry):
         cut = pl.ds(pl.multiple_of(i * 256, 256), 256)
@@ -295,86 +329,114 @@
 
     lax.fori_loop(0, D // 256, tok_turn, 0)
 
-    for h in range(NH):
-        vbuf[h, :, HD:W] = jnp.ones((T, HD), BF16)
-    loads[7].wait()
-    loads[8].wait()
-
-    def up(yy, xx):
-        block = jnp.concatenate([lat[yy, xx, k] for k in range(4)], axis=1)
-        kbuf[...] = nn(block, wkv[:, 0:W]).astype(BF16)
-        values = nn(block, wkv[:, W : 2 * W]).astype(BF16)
+    for copy in loads[7:]:
+        copy.wait()
+    wvt[...] = jnp.transpose(wv[...])
+    for h in range(NH):
+        vt[h, HD:, :] = jnp.ones((ONES, 2 * T), BF16)
+
+    def attend(blocks, masked=False):
+        keys = T * len(blocks)
+        arrays = []
+        for n, (yy, xx) in enumerate(blocks):
+            block = jnp.concatenate([lat[yy, xx, k] for k in range(4)], axis=1)
+            kbuf[n * T : (n + 1) * T, :] = nn(block, wk[...]).astype(BF16)
+            arrays.append(block)
+        scores = [
+            nt(kbuf[0:keys, h * HD : (h + 1) * HD], qbuf[:, h * HD : (h + 1) * HD]) for h in range(NH)
+        ]
+        for n, block in enumerate(arrays):
+            values = nt(wvt[...], block).astype(BF16)
+            for h in range(NH):
+                vt[h, 0:HD, n * T : (n + 1) * T] = values[h * HD : (h + 1) * HD, :]
         for h in range(NH):
-            vbuf[h, :, 0:HD] = values[:, h * HD : (h + 1) * HD]
+            score = scores[h]
+            if masked:
+                score = jnp.where(row_at <= col_at, score, NEG_FILL)
+            best = jnp.max(score, axis=0, keepdims=True)
+            if not masked:
+                old = mrun[h : h + 1, :]
+                best = jnp.maximum(old, best)
+            weights = jnp.exp2((score - best) * EXP2_SCALE).astype(BF16)
+            part = nn(vt[h, :, 0:keys], weights)
+            if not masked:
+                part += acc[h] * jnp.exp2((old - best) * EXP2_SCALE)
+            acc[h] = part
+            mrun[h : h + 1, :] = best
 
     own_to_partner.wait_recv()
-    up(y, x)
-    for h in range(NH):
-        cols = slice(h * HD, (h + 1) * HD)
-        for part in range(4):
-            rows = slice(part * 128, (part + 1) * 128)
-            upto = (part + 1) * 128
-            scores = nt(qbuf[rows, cols], kbuf[0:upto, cols])
-            r = lax.broadcasted_iota(jnp.int32, (128, upto), 0) + part * 128
-            k = lax.broadcasted_iota(jnp.int32, (128, upto), 1)
-            scores = jnp.where(k <= r, scores, NEG_FILL)
-            best = jnp.max(scores, axis=1, keepdims=True)
-            weights = jnp.exp2((scores - best) * EXP2_SCALE).astype(BF16)
-            acc[h, rows, :] = nn(weights, vbuf[h, 0:upto, :])
-            mrun[h, rows, :] = jnp.broadcast_to(best, (128, HD))
+    attend([(y, x)], masked=True)
+
+    def place(b):
+        yy = (y + pick(b, [a[0] for a in AWAY]) + 4) % 4
+        xx = (x + pick(b, [a[1] for a in AWAY]) + 4) % 4
+        return yy, xx
+
+    def pass_on(b):
+        yy, xx = place(b)
+        for copy in other_slices(b, yy, xx):
+            copy.wait_recv()
+        to_partner(b, yy, xx).start()
+
+    pass_on(0)
+    pass_on(1)
 
     def block_step(i, carry):
-        for n, first in enumerate(LEVEL_AT):
-
-            @pl.when(i == first)
+        for n in (1, 2, 3):
+
+            @pl.when(i == LEVEL_STEP[n])
             def _():
-                for copy in levels[n]:
-                    copy.wait_recv()
-                if n < 3:
-                    for copy in levels[n + 1]:
+                arrive(n)
+                if n == 1:
+                    for copy in fwd_x:
                         copy.start()
-                last = LEVEL_AT[n + 1] if n < 3 else 15
-                for b in range(first, last):
-                    to_partner(b, *away(b)).start()
-
-        yy = (y + pick(i, [a[0] for a in AWAY]) + 4) % 4
-        xx = (x + pick(i, [a[1] for a in AWAY]) + 4) % 4
-        to_partner(i, yy, xx).wait_recv()
-
-        @pl.when(yy * 4 + xx < s)
+                if n == 3:
+                    forward_row()
+
+        @pl.when(i < 7)
         def _():
-            up(yy, xx)
-            for h in range(NH):
-                cols = slice(h * HD, (h + 1) * HD)
-                for part in range(4):
-                    rows = slice(part * 128, (part + 1) * 128)
-                    scores = nt(qbuf[rows, cols], kbuf[:, cols])
-                    old = mrun[h, rows, :]
-                    best = jnp.maximum(old, jnp.max(scores, axis=1, keepdims=True))
-                    weights = jnp.exp2((scores - best[:, 0:1]) * EXP2_SCALE).astype(BF16)
-                    factor = jnp.exp2((old - best) * EXP2_SCALE)
-                    both = jnp.concatenate([factor, factor], axis=1)
-                    acc[h, rows, :] = acc[h, rows, :] * both + nn(weights, vbuf[h])
-                    mrun[h, rows, :] = best
+            pass_on(2 * i + 2)
+
+        @pl.when(i < 6)
+        def _():
+            pass_on(2 * i + 3)
+
+        y1, x1 = place(2 * i)
+        to_partner(2 * i, y1, x1).wait_recv()
+        y2, x2 = place(2 * i + 1)
+
+        @pl.when(i < 7)
+        def _():
+            to_partner(2 * i + 1, y2, x2).wait_recv()
+
+        need_1 = y1 * 4 + x1 < s
+        need_2 = jnp.logical_and(y2 * 4 + x2 < s, i < 7)
+
+        @pl.when(jnp.logical_and(need_1, need_2))
+        def _():
+            attend([(y1, x1), (y2, x2)])
+
+        @pl.when(need_1 != need_2)
+        def _():
+            attend([(jnp.where(need_1, y1, y2), jnp.where(need_1, x1, x2))])
 
         return carry
 
-    lax.fori_loop(0, 15, block_step, 0)
+    lax.fori_loop(0, 8, block_step, 0)
 
     for copy in fwd_y:
         copy.wait_recv()
     for h in range(NH):
         cols = slice(h * HD, (h + 1) * HD)
         inside_y = stage(sy, my, y, rise, h)[0]
-        inside, inside_log = row_inside[h]
-        prefix = (inside + jnp.exp(inside_log) * inside_y).astype(BF16)
+        prefix = (held[cols, :] + jnp.exp(heldlog[h : h + 1, :]) * inside_y).astype(BF16)
         sout[:, cols] = sout[:, cols] + nn(startq[:, cols], prefix)
 
     squares = jnp.zeros((8, HD), F32)
     inv = 1.0 / math.sqrt(ALL_TOKENS)
     for h in range(NH):
         cols = slice(h * HD, (h + 1) * HD)
-        teacher = (acc[h, :, 0:HD] / acc[h, :, HD:W]).astype(BF16)
+        teacher = jnp.transpose(acc[h, 0:HD, :] / acc[h, HD : HD + 1, :]).astype(BF16)
         tout_ref[:, cols] = teacher
         mismatch = sout[:, cols] - teacher.astype(F32)
         squares += jnp.sum((mismatch * mismatch).reshape(T // 8, 8, HD), axis=0)
@@ -484,7 +546,9 @@
     sent += loss_x + loss_y + loss_z + [loss_c] + rs_x1 + rs_y1 + rs_y2 + rs_x2
     for level in levels:
         sent += level
-    sent += [to_partner(b, *away(b)) for b in range(15)] + [own_to_partner]
+    for b in range(15):
+        sent += [*other_slices(b, *away(b)), to_partner(b, *away(b))]
+    sent.append(own_to_partner)
     for copy in sent:
         copy.wait_send()
 
@@ -496,17 +560,19 @@
         pltpu.VMEM((D, T), BF16),
         pltpu.VMEM((HD, D), BF16),
         pltpu.VMEM((4, D, W), BF16),
-        pltpu.VMEM((LAT, 2 * W), BF16),
+        pltpu.VMEM((LAT, W), BF16),
+        pltpu.VMEM((LAT, W), BF16),
+        pltpu.VMEM((W, LAT), BF16),
         pltpu.VMEM((NH, T), F32),
         pltpu.VMEM((4, 4, 4, T, HD), BF16),
         pltpu.VMEM((T, HD), BF16),
         pltpu.VMEM((HALF, HD), BF16),
         pltpu.VMEM((HALF, HD), BF16),
+        pltpu.VMEM((2 * T, W), BF16),
+        pltpu.VMEM((NH, HD + ONES, 2 * T), BF16),
         pltpu.VMEM((T, W), BF16),
-        pltpu.VMEM((NH, T, W), BF16),
-        pltpu.VMEM((T, W), BF16),
-        pltpu.VMEM((NH, T, W), F32),
-        pltpu.VMEM((NH, T, HD), F32),
+        pltpu.VMEM((NH, HD + ONES, T), F32),
+        pltpu.VMEM((8, T), F32),
         pltpu.VMEM((T, W), BF16),
         pltpu.VMEM((T, W), BF16),
         pltpu.VMEM((T, W), BF16),
@@ -517,6 +583,8 @@
         pltpu.VMEM((T, W), BF16),
         pltpu.VMEM((T, W), BF16),
         pltpu.VMEM((T, W), BF16),
+        pltpu.VMEM((W, HD), F32),
+        pltpu.VMEM((8, HD), F32),
         pltpu.VMEM((4, W, HD), BF16),
         pltpu.VMEM((4, W, HD), BF16),
         pltpu.VMEM((4, 8, HD), F32),
@@ -531,13 +599,15 @@
         pltpu.VMEM((NH, 3, 4, 128, HD), BF16),
         pltpu.VMEM((NH, 4, 128, HD), BF16),
         pltpu.VMEM((NH, 3, 128, HD), BF16),
-        dma((9,)),
+        dma((15,)),
         dma,
         dma,
         dma((3,)),
         dma((3,)),
-        dma((32,)),
-        dma((32,)),
+        dma((40,)),
+        dma((40,)),
+        dma((30,)),
+        dma((30,)),
         dma((16,)),
         dma((16,)),
         dma((18,)),

time: 96.6 us -> 78 us (0.81)
  Pallas kernels: 90.8 us -> 72.1 us
    pallas_call x1, Pallas kernels: 90.8 us -> 72.1 us  [per_device(): pl.pallas_call(kernel, out_shape=(jax.ShapeDtypeStruct((T, W), BF16), jax...]
where the time goes in v2:
time: 78 us; the launch traced here: 77.8 us
  Pallas kernels  72.1 us (92%)
  local copies, waits for them, and re-layouts  3.24 us (4%)
  between operations  2.4 us (3%)
    pallas_call x1, Pallas kernels, per_device(): pl.pallas_call(kernel, out_shape=(jax.ShapeDtypeStruct((T, W), BF16), jax...  72.1 us
    unnamed x2, local copies, waits for them, and re-layouts  3.24 us

profile of v2, /device:TPU:0, one launch (start us, length us, event | category | flops | bytes accessed | tf_op | source)
XLA Modules:
  0.0 77.8 jit_solution(15025052824004382444)
XLA Ops:
  0.6 72.1 %shard_map.112 = (bf16[512,256]{1,0:T(8,128)(2,1)}, f32[1,1]{1,0:T(1,128)}, f32[128,256]{1,0:T(8,128)}) custom-call(bf16[512,2048]{1,0:T(8,128)(2,1)} %tok_h.1, bf16[64,2048]{1,0:T(8,128)(2,1)} %bitcast.3, bf16[2048,256]{1,0:T(8,128)(2,1)} %wq_h.1, bf16[512,256]{1,0:T(8,128)(2,1)} %wku_h.1, bf16[512,256]{1,0:T(8,128)(2,1)} %wvu_h.1, ...), custom_call_target="tpu_custom_call" | custom-call | tf_op jit(solution)/shard_map/pallas_call | solution.py:621
  72.8 1.7 %copy.15 = bf16[512,256]{1,0:T(8,128)(2,1)} copy(bf16[512,256]{1,0:T(8,128)(2,1)} %get-tuple-element.12) | data formatting | bytes 524288
  75.1 1.6 %copy.17 = f32[128,256]{1,0:T(8,128)} copy(f32[128,256]{1,0:T(8,128)} %get-tuple-element.14) | data formatting | bytes 262144

commit v3 on v2

--- a/solution.py
+++ b/solution.py
@@ -27,11 +27,12 @@
 
 AWAY = (
     (-1, 0), (1, 0), (0, -1), (0, 1),
-    (2, 0), (-1, -1), (1, -1), (-1, 1), (1, 1), (0, 2),
+    (-1, -1), (1, -1), (-1, 1), (1, 1),
+    (2, 0), (0, 2),
     (-1, 2), (1, 2), (2, -1), (2, 1),
     (2, 2),
 )
-LEVEL_BLOCKS = ((0, 4), (4, 10), (10, 14), (14, 15))
+LEVEL_OVER_Z = ((0, 4), (4, 8), (10, 14), (14, 15))
 LEVEL_STEP = (None, 0, 2, 3)
 
 
@@ -199,7 +200,7 @@
     def row_sends(buf, sems, first, peer_of, slot):
         return [
             remote(buf.at[slot], buf.at[slot], sems[0].at[first + d - 1], sems[1].at[first + d - 1], peer_of(d))
-            for d in (1, 2, 3)
+            for d in (2, 1, 3)
         ]
 
     st = (st_s, st_r)
@@ -212,8 +213,8 @@
         sq[:, cols] = unit_q.astype(BF16)
         startq[:, cols] = (unit_q * jnp.exp(ccol[h])).astype(BF16)
 
-    def piece(idx, yy, xx, lo, size, to):
-        ref = lat.at[yy % 4, xx % 4, 0:2, pl.ds(pl.multiple_of(hb + lo, 64), size), :]
+    def piece(idx, yy, xx, lo, size, to, slots=slice(0, 2)):
+        ref = lat.at[yy % 4, xx % 4, slots, pl.ds(pl.multiple_of(hb + lo, 64), size), :]
         return remote(ref, ref, gs.at[idx], gr.at[idx], to)
 
     level_2 = [
@@ -250,6 +251,9 @@
         piece(30, y + 2, x - 1, 128, 64, xp),
         piece(31, y + 2, x + 1, 192, 64, xm),
     ]
+    rest = slice(2, 4)
+    rest_y = [piece(40, y - 1, x, 0, 128, yp, rest), piece(41, y + 1, x, 128, 128, ym, rest)]
+    rest_x = [piece(42, y, x - 1, 0, 128, xp, rest), piece(43, y, x + 1, 128, 128, xm, rest)]
     levels = (sum(level_1, []), level_2, level_3, level_4)
 
     def to_partner(i, yy, xx):
@@ -268,7 +272,7 @@
         if n < 3:
             for copy in levels[n + 1]:
                 copy.start()
-        for b in range(*LEVEL_BLOCKS[n]):
+        for b in range(*LEVEL_OVER_Z[n]):
             for copy in other_slices(b, *away(b)):
                 copy.start()
 
@@ -380,6 +384,8 @@
 
     pass_on(0)
     pass_on(1)
+    for copy in rest_y:
+        copy.start()
 
     def block_step(i, carry):
         for n in (1, 2, 3):
@@ -393,13 +399,25 @@
                 if n == 3:
                     forward_row()
 
-        @pl.when(i < 7)
+        @pl.when(jnp.logical_and(i < 7, i != 3))
         def _():
             pass_on(2 * i + 2)
 
-        @pl.when(i < 6)
+        @pl.when(jnp.logical_and(i < 6, i != 3))
         def _():
             pass_on(2 * i + 3)
+
+        @pl.when(i == 0)
+        def _():
+            for copy in rest_x:
+                copy.start()
+
+        @pl.when(i == 3)
+        def _():
+            for b, copies in ((8, rest_y), (9, rest_x)):
+                for copy in copies:
+                    copy.wait_recv()
+                to_partner(b, *away(b)).start()
 
         y1, x1 = place(2 * i)
         to_partner(2 * i, y1, x1).wait_recv()
@@ -432,6 +450,13 @@
         prefix = (held[cols, :] + jnp.exp(heldlog[h : h + 1, :]) * inside_y).astype(BF16)
         sout[:, cols] = sout[:, cols] + nn(startq[:, cols], prefix)
 
+    def head_sends(buf, first, peer_of, slot, h):
+        ref = buf.at[slot, h * HD : (h + 1) * HD, :]
+        at = [first + 3 * h + d - 1 for d in (2, 1, 3)]
+        return [remote(ref, ref, st_s.at[k], st_r.at[k], peer_of(d)) for k, d in zip(at, (2, 1, 3))]
+
+    back_x = [head_sends(bx, 12, x_peer, x, h) for h in range(NH)]
+    back_y = [head_sends(by, 18, y_peer, y, h) for h in range(NH)]
     squares = jnp.zeros((8, HD), F32)
     inv = 1.0 / math.sqrt(ALL_TOKENS)
     for h in range(NH):
@@ -441,61 +466,65 @@
         mismatch = sout[:, cols] - teacher.astype(F32)
         squares += jnp.sum((mismatch * mismatch).reshape(T // 8, 8, HD), axis=0)
         vg[:, cols] = (mismatch * inv).astype(BF16)
-    for h in range(NH):
-        cols = slice(h * HD, (h + 1) * HD)
         bx[x, cols, :] = tn(startq[:, cols], vg[:, cols]).astype(BF16)
+        for copy in back_x[h]:
+            copy.start()
     lx[x] = squares
     ls = (ls_s, ls_r)
-    back_x = row_sends(bx, st, 12, x_peer, x)
     loss_x = row_sends(lx, ls, 0, x_peer, x)
-    for copy in back_x + loss_x:
+    for copy in loss_x:
         copy.start()
     for h in range(NH):
         cols = slice(h * HD, (h + 1) * HD)
         sout[:, cols] = tn(mix[h], vg[:, cols])
 
-    for copy in back_x:
-        copy.wait_recv()
     row_inside = []
     for h in range(NH):
+        for copy in back_x[h]:
+            copy.wait_recv()
         inside, inside_log, running, _ = stage(bx, mx, x, fall, h)
         row_inside.append((inside, inside_log))
         by[y, h * HD : (h + 1) * HD, :] = running.astype(BF16)
-    back_y = row_sends(by, st, 15, y_peer, y)
-    for copy in back_y:
-        copy.start()
+        for copy in back_y[h]:
+            copy.start()
     for copy in loss_x:
         copy.wait_recv()
     ly[y] = lx[0] + lx[1] + lx[2] + lx[3]
     loss_y = row_sends(ly, ls, 3, y_peer, y)
     for copy in loss_y:
         copy.start()
-    for copy in back_y:
-        copy.wait_recv()
-    for h in range(NH):
-        cols = slice(h * HD, (h + 1) * HD)
+
+    def value_gradient(h):
+        cols = slice(h * HD, (h + 1) * HD)
+        for copy in back_y[h]:
+            copy.wait_recv()
         inside_y = stage(by, my, y, fall, h)[0]
         inside, inside_log = row_inside[h]
         suffix = (inside + jnp.exp(inside_log) * inside_y).astype(BF16)
         vg[:, cols] = (sout[:, cols] + nn(endk[:, cols], suffix)).astype(BF16)
 
-    def wgrad(i, carry):
-        part = nn(tokt[pl.ds(pl.multiple_of(i * 512, 512), 512), :], vg[...]).astype(BF16)
-        for k in range(4):
-            for h in range(NH):
-                pw[h, i, k] = part[k * 128 : (k + 1) * 128, h * HD : (h + 1) * HD]
-        return carry
-
-    lax.fori_loop(0, 4, wgrad, 0)
+    def weight_gradient(h):
+        values = vg[:, h * HD : (h + 1) * HD]
+        for i in range(4):
+            part = nn(tokt[i * 512 : (i + 1) * 512, :], values).astype(BF16)
+            for k in range(4):
+                pw[h, i, k] = part[k * 128 : (k + 1) * 128, :]
+
     rs_x1 = [
         remote(pw.at[0, :, (x + d) % 4], r1in.at[0, d - 1], rs_s.at[d - 1], rs_r.at[d - 1], x_peer(d))
-        for d in (1, 2, 3)
+        for d in (2, 1, 3)
     ]
     rs_y1 = [
         remote(pw.at[1, (y + d) % 4], r1in.at[1, d - 1], rs_s.at[d + 2], rs_r.at[d + 2], y_peer(d))
-        for d in (1, 2, 3)
-    ]
-    for copy in rs_x1 + rs_y1:
+        for d in (2, 1, 3)
+    ]
+    value_gradient(0)
+    weight_gradient(0)
+    for copy in rs_x1:
+        copy.start()
+    value_gradient(1)
+    weight_gradient(1)
+    for copy in rs_y1:
         copy.start()
     for copy in loss_y:
         copy.wait_recv()
@@ -511,7 +540,7 @@
         r1own[0, k] = (mine[k] + sum(r1in[0, d, k].astype(F32) for d in range(3))).astype(BF16)
     rs_y2 = [
         remote(r1own.at[0, (y + d) % 4], r2in.at[0, d - 1], rs_s.at[d + 5], rs_r.at[d + 5], y_peer(d))
-        for d in (1, 2, 3)
+        for d in (2, 1, 3)
     ]
     for copy in rs_y2:
         copy.start()
@@ -522,7 +551,7 @@
         r1own[1, k] = (mine[k] + sum(r1in[1, d, k].astype(F32) for d in range(3))).astype(BF16)
     rs_x2 = [
         remote(r1own.at[1, (x + d) % 4], r2in.at[1, d - 1], rs_s.at[d + 8], rs_r.at[d + 8], x_peer(d))
-        for d in (1, 2, 3)
+        for d in (2, 1, 3)
     ]
     for copy in rs_x2:
         copy.start()
@@ -542,15 +571,30 @@
         copy.wait_recv()
     wg_ref[:, HD:W] = r1own[1, x].astype(F32) + sum(r2in[1, d].astype(F32) for d in range(3))
 
-    sent = [to_pair] + to_z + fwd_x + fwd_y + back_x + back_y
+    sent = [to_pair] + to_z + fwd_x + fwd_y + sum(back_x + back_y, [])
     sent += loss_x + loss_y + loss_z + [loss_c] + rs_x1 + rs_y1 + rs_y2 + rs_x2
     for level in levels:
         sent += level
     for b in range(15):
-        sent += [*other_slices(b, *away(b)), to_partner(b, *away(b))]
+        sent += [to_partner(b, *away(b))]
+    for first, last in LEVEL_OVER_Z:
+        for b in range(first, last):
+            sent += other_slices(b, *away(b))
+    sent += rest_x + rest_y
     sent.append(own_to_partner)
     for copy in sent:
         copy.wait_send()
+
+
+def finish(teacher_ref, wgrad_ref, teacher_out, wgrad_out, sem):
+    copies = [
+        pltpu.make_async_copy(teacher_ref, teacher_out, sem.at[0]),
+        pltpu.make_async_copy(wgrad_ref, wgrad_out, sem.at[1]),
+    ]
+    for copy in copies:
+        copy.start()
+    for copy in copies:
+        copy.wait()
 
 
 def per_device(tokens, w_latent, w_query, w_key_up, w_value_up, w_stu_query, w_stu_key, w_stu_value, forget):
@@ -604,14 +648,14 @@
         dma,
         dma((3,)),
         dma((3,)),
-        dma((40,)),
-        dma((40,)),
+        dma((44,)),
+        dma((44,)),
         dma((30,)),
         dma((30,)),
         dma((16,)),
         dma((16,)),
-        dma((18,)),
-        dma((18,)),
+        dma((24,)),
+        dma((24,)),
         dma((12,)),
         dma((12,)),
         dma((10,)),
@@ -621,9 +665,9 @@
     teacher, loss, wgrad = pl.pallas_call(
         kernel,
         out_shape=(
-            jax.ShapeDtypeStruct((T, W), BF16),
+            pltpu.VMEM((T, W), BF16),
             jax.ShapeDtypeStruct((1, 1), F32),
-            jax.ShapeDtypeStruct((128, W), F32),
+            pltpu.VMEM((128, W), F32),
         ),
         in_specs=[anywhere] * 9,
         out_specs=(
@@ -638,6 +682,14 @@
     )(
         tokens, w_latent.T, w_query, w_key_up, w_value_up, w_stu_query, w_stu_key, w_stu_value, forget.T
     )
+    teacher, wgrad = pl.pallas_call(
+        finish,
+        out_shape=(jax.ShapeDtypeStruct((T, W), BF16), jax.ShapeDtypeStruct((128, W), F32)),
+        in_specs=[pl.BlockSpec(memory_space=pltpu.VMEM)] * 2,
+        out_specs=(anywhere, anywhere),
+        scratch_shapes=[dma((2,))],
+        compiler_params=pltpu.CompilerParams(vmem_limit_bytes=4 * 1024 * 1024),
+    )(teacher, wgrad)
     return teacher, loss[0, 0], wgrad
 
 

time: 78 us -> 72.1 us (0.924)
  local copies, waits for them, and re-layouts: 3.24 us -> 0 us
  Pallas kernels: 72.1 us -> 69.4 us
    unnamed x2 -> x0, local copies, waits for them, and re-layouts: 3.24 us -> none
    pallas_call x1 -> x2, Pallas kernels: 72.1 us -> 69.4 us  [the longest x1 68.6 us: per_device(): pl.pallas_call(kernel, out_shape=(pltpu.VMEM((T, W), BF16), jax.ShapeDtyp...]
where the time goes in v3:
time: 72.1 us; the launch traced here: 71.8 us
  Pallas kernels  69.4 us (96%)
  between operations  2.41 us (3%)
    pallas_call x1, Pallas kernels, per_device(): pl.pallas_call(kernel, out_shape=(pltpu.VMEM((T, W), BF16), jax.ShapeDtyp...  68.6 us

profile of v3, /device:TPU:0, one launch (start us, length us, event | category | flops | bytes accessed | tf_op | source)
XLA Modules:
  0.0 71.8 jit_solution(1030879020415937216)
XLA Ops:
  0.6 68.6 %shard_map.112 = (bf16[512,256]{1,0:T(8,128)(2,1)S(1)}, f32[1,1]{1,0:T(1,128)}, f32[128,256]{1,0:T(8,128)S(1)}) custom-call(bf16[512,2048]{1,0:T(8,128)(2,1)} %tok_h.1, bf16[64,2048]{1,0:T(8,128)(2,1)} %bitcast.3, bf16[2048,256]{1,0:T(8,128)(2,1)} %wq_h.1, bf16[512,256]{1,0:T(8,128)(2,1)} %wku_h.1, bf16[512,256]{1,0:T(8,128)(2,1)} %wvu_h.1, ...), custom_call_target="tpu_custom_call" | custom-call | tf_op jit(solution)/shard_map/pallas_call | solution.py:665
  69.3 0.8 %shard_map.113 = (bf16[512,256]{1,0:T(8,128)(2,1)}, f32[128,256]{1,0:T(8,128)}) custom-call(bf16[512,256]{1,0:T(8,128)(2,1)S(1)} %get-tuple-element.8.teacher_ref, f32[128,256]{1,0:T(8,128)S(1)} %get-tuple-element.9.wgrad_ref), custom_call_target="tpu_custom_call" | custom-call | tf_op jit(solution)/shard_map/pallas_call | solution.py:685

commit v4 on v3

--- a/solution.py
+++ b/solution.py
@@ -33,7 +33,7 @@
     (2, 2),
 )
 LEVEL_OVER_Z = ((0, 4), (4, 8), (10, 14), (14, 15))
-LEVEL_STEP = (None, 0, 2, 3)
+LEVEL_STEP = (None, None, 2, 4)
 
 
 def nt(a, b):
@@ -70,9 +70,9 @@
     lat, myp, pairin, pairbuf, kbuf, vt, qbuf, acc, mrun,
     sq, sk, sv, ccol, crow, mix, sout, startq, endk, vg,
     held, heldlog, sx, sy, mx, my, bx, by, lx, ly, lz, lc,
-    pw, r1in, r1own, r2in,
+    pw, r1in, r1own, r2in, gw, gwin, hrow, lown, lin,
     load_sem, pair_s, pair_r, z_s, z_r, gs, gr, zg_s, zg_r, ds_, dr,
-    st_s, st_r, rs_s, rs_r, ls_s, ls_r,
+    st_s, st_r, rs_s, rs_r, ls_s, ls_r, gw_s, gw_r,
 ):
     s = lax.axis_index("seq")
     t = lax.axis_index("tensor")
@@ -204,7 +204,10 @@
         ]
 
     st = (st_s, st_r)
-    fwd_x = row_sends(sx, st, 0, x_peer, x) + row_sends(mx, st, 3, x_peer, x)
+    fwd_x = row_sends(sx, st, 0, x_peer, x)
+    ends_x = row_sends(mx, st, 3, x_peer, x)
+    for copy in ends_x:
+        copy.start()
     loads[5].wait()
     queries_f = project(3)
     for h in range(NH):
@@ -382,20 +385,39 @@
             copy.wait_recv()
         to_partner(b, yy, xx).start()
 
+    for copy in ends_x:
+        copy.wait_recv()
+    for h in range(NH):
+        cols = slice(h * HD, (h + 1) * HD)
+        to_end = sum(jnp.where(x < k, mx[k, h : h + 1, :], 0.0) for k in (1, 2, 3))
+        faded = (endk[:, cols].astype(F32) * jnp.exp(to_end)).astype(BF16)
+        for i in range(4):
+            part = nn(tokt[i * 512 : (i + 1) * 512, :], faded).astype(BF16)
+            for k in range(4):
+                gw[h, i, k] = part[k * 128 : (k + 1) * 128, :]
+    row_gw = [
+        [
+            remote(gw.at[h, :, (x + d) % 4], gwin.at[h, d - 1], gw_s.at[3 * h + d - 1], gw_r.at[3 * h + d - 1], x_peer(d))
+            for d in (2, 1, 3)
+        ]
+        for h in range(NH)
+    ]
+    arrive(1)
+    for copy in fwd_x:
+        copy.start()
     pass_on(0)
     pass_on(1)
     for copy in rest_y:
         copy.start()
 
     def block_step(i, carry):
-        for n in (1, 2, 3):
+        for n in (2, 3):
 
             @pl.when(i == LEVEL_STEP[n])
             def _():
                 arrive(n)
-                if n == 1:
-                    for copy in fwd_x:
-                        copy.start()
+                for copy in row_gw[n - 2]:
+                    copy.start()
                 if n == 3:
                     forward_row()
 
@@ -478,12 +500,18 @@
         cols = slice(h * HD, (h + 1) * HD)
         sout[:, cols] = tn(mix[h], vg[:, cols])
 
+    for h in range(NH):
+        for copy in row_gw[h]:
+            copy.wait_recv()
+        for k in range(4):
+            total = gw[h, k, x].astype(F32) + sum(gwin[h, d, k].astype(F32) for d in range(3))
+            hrow[h, k * 128 : (k + 1) * 128, :] = total.astype(BF16)
     row_inside = []
     for h in range(NH):
         for copy in back_x[h]:
             copy.wait_recv()
         inside, inside_log, running, _ = stage(bx, mx, x, fall, h)
-        row_inside.append((inside, inside_log))
+        row_inside.append(inside.astype(BF16))
         by[y, h * HD : (h + 1) * HD, :] = running.astype(BF16)
         for copy in back_y[h]:
             copy.start()
@@ -496,12 +524,12 @@
 
     def value_gradient(h):
         cols = slice(h * HD, (h + 1) * HD)
+        vg[:, cols] = (sout[:, cols] + nn(endk[:, cols], row_inside[h])).astype(BF16)
+
+    def from_later_rows(h):
         for copy in back_y[h]:
             copy.wait_recv()
-        inside_y = stage(by, my, y, fall, h)[0]
-        inside, inside_log = row_inside[h]
-        suffix = (inside + jnp.exp(inside_log) * inside_y).astype(BF16)
-        vg[:, cols] = (sout[:, cols] + nn(endk[:, cols], suffix)).astype(BF16)
+        return nn(hrow[h], stage(by, my, y, fall, h)[0].astype(BF16))
 
     def weight_gradient(h):
         values = vg[:, h * HD : (h + 1) * HD]
@@ -526,6 +554,15 @@
     weight_gradient(1)
     for copy in rs_y1:
         copy.start()
+    later = from_later_rows(0)
+    later_1 = from_later_rows(1)
+    for k in range(4):
+        lown[k] = later_1[k * 128 : (k + 1) * 128, :].astype(BF16)
+    rows_y = [
+        remote(lown.at[(y + d) % 4], lin.at[d - 1], rs_s.at[d + 11], rs_r.at[d + 11], y_peer(d)) for d in (2, 1, 3)
+    ]
+    for copy in rows_y:
+        copy.start()
     for copy in loss_y:
         copy.wait_recv()
     lz[z] = ly[0] + ly[1] + ly[2] + ly[3]
@@ -537,7 +574,8 @@
         copy.wait_recv()
     mine = [pw[0, k, x].astype(F32) for k in range(4)]
     for k in range(4):
-        r1own[0, k] = (mine[k] + sum(r1in[0, d, k].astype(F32) for d in range(3))).astype(BF16)
+        total = mine[k] + later[k * 128 : (k + 1) * 128, :]
+        r1own[0, k] = (total + sum(r1in[0, d, k].astype(F32) for d in range(3))).astype(BF16)
     rs_y2 = [
         remote(r1own.at[0, (y + d) % 4], r2in.at[0, d - 1], rs_s.at[d + 5], rs_r.at[d + 5], y_peer(d))
         for d in (2, 1, 3)
@@ -567,12 +605,16 @@
     for copy in rs_y2:
         copy.wait_recv()
     wg_ref[:, 0:HD] = r1own[0, y].astype(F32) + sum(r2in[0, d].astype(F32) for d in range(3))
+    for copy in rows_y:
+        copy.wait_recv()
+    late = lown[y].astype(F32) + sum(lin[d].astype(F32) for d in range(3))
     for copy in rs_x2:
         copy.wait_recv()
-    wg_ref[:, HD:W] = r1own[1, x].astype(F32) + sum(r2in[1, d].astype(F32) for d in range(3))
+    wg_ref[:, HD:W] = late + r1own[1, x].astype(F32) + sum(r2in[1, d].astype(F32) for d in range(3))
 
     sent = [to_pair] + to_z + fwd_x + fwd_y + sum(back_x + back_y, [])
     sent += loss_x + loss_y + loss_z + [loss_c] + rs_x1 + rs_y1 + rs_y2 + rs_x2
+    sent += ends_x + sum(row_gw, []) + rows_y
     for level in levels:
         sent += level
     for b in range(15):
@@ -643,6 +685,11 @@
         pltpu.VMEM((NH, 3, 4, 128, HD), BF16),
         pltpu.VMEM((NH, 4, 128, HD), BF16),
         pltpu.VMEM((NH, 3, 128, HD), BF16),
+        pltpu.VMEM((NH, 4, 4, 128, HD), BF16),
+        pltpu.VMEM((NH, 3, 4, 128, HD), BF16),
+        pltpu.VMEM((NH, 512, HD), BF16),
+        pltpu.VMEM((4, 128, HD), BF16),
+        pltpu.VMEM((3, 128, HD), BF16),
         dma((15,)),
         dma,
         dma,
@@ -656,10 +703,12 @@
         dma((16,)),
         dma((24,)),
         dma((24,)),
-        dma((12,)),
-        dma((12,)),
+        dma((15,)),
+        dma((15,)),
         dma((10,)),
         dma((10,)),
+        dma((6,)),
+        dma((6,)),
     ]
     anywhere = pl.BlockSpec(memory_space=pl.ANY)
     teacher, loss, wgrad = pl.pallas_call(

time: 72.1 us -> 69.9 us (0.969)
  Pallas kernels: 69.4 us -> 67.3 us
    pallas_call x1, Pallas kernels: 68.6 us -> 66.6 us  [per_device(): pl.pallas_call(kernel, out_shape=(pltpu.VMEM((T, W), BF16), jax.ShapeDtyp...]
where the time goes in v4:
time: 69.9 us; the launch traced here: 69.8 us
  Pallas kernels  67.3 us (96%)
  between operations  2.41 us (3%)
    pallas_call x1, Pallas kernels, per_device(): pl.pallas_call(kernel, out_shape=(pltpu.VMEM((T, W), BF16), jax.ShapeDtyp...  66.6 us

profile of v4, /device:TPU:0, one launch (start us, length us, event | category | flops | bytes accessed | tf_op | source)
XLA Modules:
  0.0 69.8 jit_solution(340834558729993823)
XLA Ops:
  0.6 66.6 %shard_map.112 = (bf16[512,256]{1,0:T(8,128)(2,1)S(1)}, f32[1,1]{1,0:T(1,128)}, f32[128,256]{1,0:T(8,128)S(1)}) custom-call(bf16[512,2048]{1,0:T(8,128)(2,1)} %tok_h.1, bf16[64,2048]{1,0:T(8,128)(2,1)} %bitcast.3, bf16[2048,256]{1,0:T(8,128)(2,1)} %wq_h.1, bf16[512,256]{1,0:T(8,128)(2,1)} %wku_h.1, bf16[512,256]{1,0:T(8,128)(2,1)} %wvu_h.1, ...), custom_call_target="tpu_custom_call" | custom-call | tf_op jit(solution)/shard_map/pallas_call | solution.py:714
  67.2 0.8 %shard_map.113 = (bf16[512,256]{1,0:T(8,128)(2,1)}, f32[128,256]{1,0:T(8,128)}) custom-call(bf16[512,256]{1,0:T(8,128)(2,1)S(1)} %get-tuple-element.8.teacher_ref, f32[128,256]{1,0:T(8,128)S(1)} %get-tuple-element.9.wgrad_ref), custom_call_target="tpu_custom_call" | custom-call | tf_op jit(solution)/shard_map/pallas_call | solution.py:734

commit v5 on v4

--- a/solution.py
+++ b/solution.py
@@ -21,19 +21,19 @@
 LAT = 512
 HALF = T // 2
 ONES = 16
+NA = 32
 ALL_TOKENS = 8192
 ALL_HEADS = 16
 EXP2_SCALE = math.log2(math.e) / math.sqrt(HD)
 
 AWAY = (
     (-1, 0), (1, 0), (0, -1), (0, 1),
-    (-1, -1), (1, -1), (-1, 1), (1, 1),
-    (2, 0), (0, 2),
+    (-1, -1), (1, -1), (2, 0), (0, 2), (-1, 1), (1, 1),
     (-1, 2), (1, 2), (2, -1), (2, 1),
     (2, 2),
 )
-LEVEL_OVER_Z = ((0, 4), (4, 8), (10, 14), (14, 15))
-LEVEL_STEP = (None, None, 2, 4)
+LEVEL_OVER_Z = ((0, 1, 2, 3), (4, 5, 8, 9), (10, 11, 12, 13), (14,))
+LEVEL_STEP = 4
 
 
 def nt(a, b):
@@ -70,7 +70,7 @@
     lat, myp, pairin, pairbuf, kbuf, vt, qbuf, acc, mrun,
     sq, sk, sv, ccol, crow, mix, sout, startq, endk, vg,
     held, heldlog, sx, sy, mx, my, bx, by, lx, ly, lz, lc,
-    pw, r1in, r1own, r2in, gw, gwin, hrow, lown, lin,
+    pw, r1in, r1own, r2in, gw, gwin, hrow, lown, lin, a1in, a1own, a2in,
     load_sem, pair_s, pair_r, z_s, z_r, gs, gr, zg_s, zg_r, ds_, dr,
     st_s, st_r, rs_s, rs_r, ls_s, ls_r, gw_s, gw_r,
 ):
@@ -275,7 +275,7 @@
         if n < 3:
             for copy in levels[n + 1]:
                 copy.start()
-        for b in range(*LEVEL_OVER_Z[n]):
+        for b in LEVEL_OVER_Z[n]:
             for copy in other_slices(b, *away(b)):
                 copy.start()
 
@@ -411,21 +411,25 @@
         copy.start()
 
     def block_step(i, carry):
-        for n in (2, 3):
-
-            @pl.when(i == LEVEL_STEP[n])
+        @pl.when(i == LEVEL_STEP)
+        def _():
+            arrive(3)
+            forward_row()
+
+        for h, step in ((0, 3), (1, 4)):
+
+            @pl.when(i == step)
             def _():
-                arrive(n)
-                for copy in row_gw[n - 2]:
+                for copy in row_gw[h]:
                     copy.start()
-                if n == 3:
-                    forward_row()
-
-        @pl.when(jnp.logical_and(i < 7, i != 3))
+
+        ahead = jnp.logical_or(i == 0, i >= 3)
+
+        @pl.when(jnp.logical_and(i < 7, ahead))
         def _():
             pass_on(2 * i + 2)
 
-        @pl.when(jnp.logical_and(i < 6, i != 3))
+        @pl.when(jnp.logical_and(i < 6, ahead))
         def _():
             pass_on(2 * i + 3)
 
@@ -434,9 +438,9 @@
             for copy in rest_x:
                 copy.start()
 
-        @pl.when(i == 3)
+        @pl.when(i == 2)
         def _():
-            for b, copies in ((8, rest_y), (9, rest_x)):
+            for b, copies in ((6, rest_y), (7, rest_x)):
                 for copy in copies:
                     copy.wait_recv()
                 to_partner(b, *away(b)).start()
@@ -459,6 +463,12 @@
         @pl.when(need_1 != need_2)
         def _():
             attend([(jnp.where(need_1, y1, y2), jnp.where(need_1, x1, x2))])
+
+        @pl.when(i == 1)
+        def _():
+            arrive(2)
+            pass_on(4)
+            pass_on(5)
 
         return carry
 
@@ -500,12 +510,6 @@
         cols = slice(h * HD, (h + 1) * HD)
         sout[:, cols] = tn(mix[h], vg[:, cols])
 
-    for h in range(NH):
-        for copy in row_gw[h]:
-            copy.wait_recv()
-        for k in range(4):
-            total = gw[h, k, x].astype(F32) + sum(gwin[h, d, k].astype(F32) for d in range(3))
-            hrow[h, k * 128 : (k + 1) * 128, :] = total.astype(BF16)
     row_inside = []
     for h in range(NH):
         for copy in back_x[h]:
@@ -543,21 +547,37 @@
         for d in (2, 1, 3)
     ]
     rs_y1 = [
-        remote(pw.at[1, (y + d) % 4], r1in.at[1, d - 1], rs_s.at[d + 2], rs_r.at[d + 2], y_peer(d))
+        remote(
+            pw.at[1, (y + d) % 4, :, NA:, :],
+            r1in.at[1, d - 1, :, NA:, :],
+            rs_s.at[d + 2],
+            rs_r.at[d + 2],
+            y_peer(d),
+        )
+        for d in (1, 3, 2)
+    ]
+    rs_a1 = [
+        remote(pw.at[1, :, (x + d) % 4, 0:NA, :], a1in.at[d - 1], rs_s.at[d + 14], rs_r.at[d + 14], x_peer(d))
         for d in (2, 1, 3)
     ]
     value_gradient(0)
+    value_gradient(1)
+    weight_gradient(1)
+    for copy in rs_y1 + rs_a1:
+        copy.start()
     weight_gradient(0)
     for copy in rs_x1:
         copy.start()
-    value_gradient(1)
-    weight_gradient(1)
-    for copy in rs_y1:
-        copy.start()
+    for h in range(NH):
+        for copy in row_gw[h]:
+            copy.wait_recv()
+        for k in range(4):
+            total = gw[h, k, x].astype(F32) + sum(gwin[h, d, k].astype(F32) for d in range(3))
+            hrow[h, k * 128 : (k + 1) * 128, :] = total.astype(BF16)
     later = from_later_rows(0)
     later_1 = from_later_rows(1)
     for k in range(4):
-        lown[k] = later_1[k * 128 : (k + 1) * 128, :].astype(BF16)
+        lown[k] = later_1[k * 128 + NA : (k + 1) * 128, :].astype(BF16)
     rows_y = [
         remote(lown.at[(y + d) % 4], lin.at[d - 1], rs_s.at[d + 11], rs_r.at[d + 11], y_peer(d)) for d in (2, 1, 3)
     ]
@@ -582,13 +602,30 @@
     ]
     for copy in rs_y2:
         copy.start()
+    for copy in rs_a1:
+        copy.wait_recv()
+    for k in range(4):
+        total = pw[1, k, x, 0:NA, :].astype(F32) + later_1[k * 128 : k * 128 + NA, :]
+        a1own[k] = (total + sum(a1in[d, k].astype(F32) for d in range(3))).astype(BF16)
+    rs_a2 = [
+        remote(a1own.at[(y + d) % 4], a2in.at[d - 1], rs_s.at[d + 17], rs_r.at[d + 17], y_peer(d)) for d in (2, 1, 3)
+    ]
+    for copy in rs_a2:
+        copy.start()
     for copy in rs_y1:
         copy.wait_recv()
-    mine = [pw[1, y, k].astype(F32) for k in range(4)]
+    mine = [pw[1, y, k, NA:, :].astype(F32) for k in range(4)]
     for k in range(4):
-        r1own[1, k] = (mine[k] + sum(r1in[1, d, k].astype(F32) for d in range(3))).astype(BF16)
+        total = mine[k] + sum(r1in[1, d, k, NA:, :].astype(F32) for d in range(3))
+        r1own[1, k, NA:, :] = total.astype(BF16)
     rs_x2 = [
-        remote(r1own.at[1, (x + d) % 4], r2in.at[1, d - 1], rs_s.at[d + 8], rs_r.at[d + 8], x_peer(d))
+        remote(
+            r1own.at[1, (x + d) % 4, NA:, :],
+            r2in.at[1, d - 1, NA:, :],
+            rs_s.at[d + 8],
+            rs_r.at[d + 8],
+            x_peer(d),
+        )
         for d in (2, 1, 3)
     ]
     for copy in rs_x2:
@@ -610,17 +647,21 @@
     late = lown[y].astype(F32) + sum(lin[d].astype(F32) for d in range(3))
     for copy in rs_x2:
         copy.wait_recv()
-    wg_ref[:, HD:W] = late + r1own[1, x].astype(F32) + sum(r2in[1, d].astype(F32) for d in range(3))
+    partial = r1own[1, x, NA:, :].astype(F32) + sum(r2in[1, d, NA:, :].astype(F32) for d in range(3))
+    wg_ref[NA:, HD:W] = late + partial
+    for copy in rs_a2:
+        copy.wait_recv()
+    wg_ref[0:NA, HD:W] = a1own[y].astype(F32) + sum(a2in[d].astype(F32) for d in range(3))
 
     sent = [to_pair] + to_z + fwd_x + fwd_y + sum(back_x + back_y, [])
     sent += loss_x + loss_y + loss_z + [loss_c] + rs_x1 + rs_y1 + rs_y2 + rs_x2
-    sent += ends_x + sum(row_gw, []) + rows_y
+    sent += rs_a1 + rs_a2 + ends_x + sum(row_gw, []) + rows_y
     for level in levels:
         sent += level
     for b in range(15):
         sent += [to_partner(b, *away(b))]
-    for first, last in LEVEL_OVER_Z:
-        for b in range(first, last):
+    for blocks in LEVEL_OVER_Z:
+        for b in blocks:
             sent += other_slices(b, *away(b))
     sent += rest_x + rest_y
     sent.append(own_to_partner)
@@ -688,8 +729,11 @@
         pltpu.VMEM((NH, 4, 4, 128, HD), BF16),
         pltpu.VMEM((NH, 3, 4, 128, HD), BF16),
         pltpu.VMEM((NH, 512, HD), BF16),
-        pltpu.VMEM((4, 128, HD), BF16),
-        pltpu.VMEM((3, 128, HD), BF16),
+        pltpu.VMEM((4, 128 - NA, HD), BF16),
+        pltpu.VMEM((3, 128 - NA, HD), BF16),
+        pltpu.VMEM((3, 4, NA, HD), BF16),
+        pltpu.VMEM((4, NA, HD), BF16),
+        pltpu.VMEM((3, NA, HD), BF16),
         dma((15,)),
         dma,
         dma,
@@ -703,8 +747,8 @@
         dma((16,)),
         dma((24,)),
         dma((24,)),
-        dma((15,)),
-        dma((15,)),
+        dma((21,)),
+        dma((21,)),
         dma((10,)),
         dma((10,)),
         dma((6,)),

time: 69.9 us -> 69.9 us (level)
  no operation moved by 1% of the time
where the time goes in v5:
time: 69.9 us; the launch traced here: 69.8 us
  Pallas kernels  67.4 us (96%)
  between operations  2.41 us (3%)
    pallas_call x1, Pallas kernels, per_device(): pl.pallas_call(kernel, out_shape=(pltpu.VMEM((T, W), BF16), jax.ShapeDtyp...  66.6 us

profile of v5, /device:TPU:0, one launch (start us, length us, event | category | flops | bytes accessed | tf_op | source)
XLA Modules:
  0.0 69.8 jit_solution(4507215838505560324)
XLA Ops:
  0.6 66.6 %shard_map.112 = (bf16[512,256]{1,0:T(8,128)(2,1)S(1)}, f32[1,1]{1,0:T(1,128)}, f32[128,256]{1,0:T(8,128)S(1)}) custom-call(bf16[512,2048]{1,0:T(8,128)(2,1)} %tok_h.1, bf16[64,2048]{1,0:T(8,128)(2,1)} %bitcast.3, bf16[2048,256]{1,0:T(8,128)(2,1)} %wq_h.1, bf16[512,256]{1,0:T(8,128)(2,1)} %wku_h.1, bf16[512,256]{1,0:T(8,128)(2,1)} %wvu_h.1, ...), custom_call_target="tpu_custom_call" | custom-call | tf_op jit(solution)/shard_map/pallas_call | solution.py:758
  67.2 0.8 %shard_map.113 = (bf16[512,256]{1,0:T(8,128)(2,1)}, f32[128,256]{1,0:T(8,128)}) custom-call(bf16[512,256]{1,0:T(8,128)(2,1)S(1)} %get-tuple-element.8.teacher_ref, f32[128,256]{1,0:T(8,128)S(1)} %get-tuple-element.9.wgrad_ref), custom_call_target="tpu_custom_call" | custom-call | tf_op jit(solution)/shard_map/pallas_call | solution.py:778

commit v6 on v5

--- a/solution.py
+++ b/solution.py
@@ -21,7 +21,7 @@
 LAT = 512
 HALF = T // 2
 ONES = 16
-NA = 32
+NA = 16
 ALL_TOKENS = 8192
 ALL_HEADS = 16
 EXP2_SCALE = math.log2(math.e) / math.sqrt(HD)

time: 69.9 us -> 70 us (level)
  no operation moved by 1% of the time
where the time goes in v6:
time: 70 us; the launch traced here: 69.3 us
  Pallas kernels  66.9 us (96%)
  between operations  2.41 us (3%)
    pallas_call x1, Pallas kernels, per_device(): pl.pallas_call(kernel, out_shape=(pltpu.VMEM((T, W), BF16), jax.ShapeDtyp...  66.1 us

profile of v6, /device:TPU:0, one launch (start us, length us, event | category | flops | bytes accessed | tf_op | source)
XLA Modules:
  0.0 69.3 jit_solution(4668690128475066571)
XLA Ops:
  0.6 66.1 %shard_map.112 = (bf16[512,256]{1,0:T(8,128)(2,1)S(1)}, f32[1,1]{1,0:T(1,128)}, f32[128,256]{1,0:T(8,128)S(1)}) custom-call(bf16[512,2048]{1,0:T(8,128)(2,1)} %tok_h.1, bf16[64,2048]{1,0:T(8,128)(2,1)} %bitcast.3, bf16[2048,256]{1,0:T(8,128)(2,1)} %wq_h.1, bf16[512,256]{1,0:T(8,128)(2,1)} %wku_h.1, bf16[512,256]{1,0:T(8,128)(2,1)} %wvu_h.1, ...), custom_call_target="tpu_custom_call" | custom-call | tf_op jit(solution)/shard_map/pallas_call | solution.py:758
  66.8 0.8 %shard_map.113 = (bf16[512,256]{1,0:T(8,128)(2,1)}, f32[128,256]{1,0:T(8,128)}) custom-call(bf16[512,256]{1,0:T(8,128)(2,1)S(1)} %get-tuple-element.8.teacher_ref, f32[128,256]{1,0:T(8,128)S(1)} %get-tuple-element.9.wgrad_ref), custom_call_target="tpu_custom_call" | custom-call | tf_op jit(solution)/shard_map/pallas_call | solution.py:778
